TPU v7x, 256 devices: a whole 4x4x8 slice. The times are simulated.
256 devices in a mesh: row: 64 (over z_hi, x, y, core), rep: 4 (over z_lo).
Axes of the slice: x: 4, y: 4, z: 8 (z_hi: 2, z_lo: 4; z = z_hi * 4 + z_lo), core: 2. Of those that a mesh axis runs over, the one named last changes fastest.
Arguments:
- features: bfloat16 [32768, 128], P('row'), may hold values from -6 to 6
- tiles: bfloat16 [4096, 4, 256, 256], P('row', 'rep'), may hold values from -0.375 to 0.375
- tile_where: int32 [4096, 4, 2], P('row', 'rep'), may hold values from 0 to 127, as said below
- tile_count: int32 [64, 4], P('row', 'rep'), may hold values from 1 to 64, as said below
- degree: int32 [32768], P('row'), may hold values from 1 to 8
- self_one: bfloat16 [128, 256], replicated, may hold values from -0.5 to 0.5
- neigh_one: bfloat16 [128, 256], replicated, may hold values from -0.5 to 0.5
- self_two: bfloat16 [256, 256], replicated, may hold values from -0.375 to 0.375
- neigh_two: bfloat16 [256, 256], replicated, may hold values from -0.375 to 0.375
Outputs:
- embedding: float32 [32768, 256], P('row')
Inputs may be any that keep to these rules, and one draw needn't show every extreme that they name: `tile_where`: column 0 is a tile row of 0 to 1, column 1 a tile column of 0 to 127. `tile_count`: some block row and replica has all 64 slots live in every draw.
All inputs are finite; a program needn't handle non-finite values.
Results may differ from a plain program's by a relative error of at most 0.005.
Values may be sent and summed in bfloat16 or wider, within the bound.
No kernel may reach another device: no remote copies, remote signals or barrier semaphores. Data moves between devices by JAX's collectives and lax.ppermute only.
A program may use at most 128 MiB of HBM per device.

v0:
```python
import jax
import jax.numpy as jnp
from jax import lax
from jax.sharding import PartitionSpec as P

TILE = 256


def cut_along(value, dim, peers):
    before, after = (value.shape[:dim], value.shape[dim + 1 :])
    return jnp.moveaxis(value.reshape(*before, peers, -1, *after), dim, 0)


def summed_on_arrival(value, axis, dim):
    peers = lax.axis_size(axis)
    pieces = lax.all_to_all(cut_along(value, dim, peers), axis, 0, 0, tiled=True)
    return jnp.sum(pieces, axis=0)


def sent_to_all(value, axis):
    peers = lax.axis_size(axis)
    return lax.all_to_all(
        jnp.broadcast_to(value[None], (peers, *value.shape)), axis, 0, 0, tiled=True
    )


def in_order(pieces, dim):
    lengths = list(pieces.shape[1:])
    lengths[dim] *= pieces.shape[0]
    return jnp.moveaxis(pieces, 0, dim).reshape(lengths)


def collect(value, axis, dim):
    pieces = sent_to_all(value, axis)
    return in_order(pieces, dim)


def spread_columns(whole):
    return lax.all_gather(whole, "row", axis=0, tiled=True)


def reduce_rows(partial_value):
    return summed_on_arrival(partial_value, "rep", 0)


def per_device(
    features, tiles, tile_where, tile_count, degree, self_one, neigh_one, self_two, neigh_two
):
    rows = features.shape[0]
    quarter = rows // lax.axis_size("rep")
    offset = lax.axis_index("rep") * quarter
    slots = tiles.shape[0]
    per_block = rows // TILE
    tile_block = tiles.reshape(slots, TILE, TILE)
    where_block = tile_where.reshape(slots, 2)
    live = jnp.arange(slots, dtype=jnp.int32) < tile_count.reshape(())
    segment = jnp.where(live, where_block[:, 0], per_block)
    column_ids = where_block[:, 1]

    def neighbour_sum(whole, width):
        gathered = spread_columns(whole)
        blocks = gathered.reshape(-1, TILE, width)
        columns = jnp.take(blocks, column_ids, axis=0)
        products = jnp.einsum(
            "sij,sjf->sif", tile_block, columns, preferred_element_type=jnp.float32
        )
        summed = jax.ops.segment_sum(products, segment, num_segments=per_block + 1)[:per_block]
        return reduce_rows(summed.reshape(rows, width))

    feature_share = lax.dynamic_slice_in_dim(features, offset, quarter, 0)
    width_in = features.shape[1]
    width_hidden = self_one.shape[1]
    scale = lax.dynamic_slice_in_dim(degree, offset, quarter, 0).astype(jnp.float32)[:, None]
    agg_one = (neighbour_sum(features, width_in) / scale).astype(jnp.bfloat16)
    first = jnp.dot(feature_share, self_one, preferred_element_type=jnp.float32) + jnp.dot(
        agg_one, neigh_one, preferred_element_type=jnp.float32
    )
    hidden_share = jax.nn.relu(first).astype(jnp.bfloat16)
    hidden = collect(hidden_share, "rep", 0)
    agg_two = (neighbour_sum(hidden, width_hidden) / scale).astype(jnp.bfloat16)
    result_share = jnp.dot(hidden_share, self_two, preferred_element_type=jnp.float32) + jnp.dot(
        agg_two, neigh_two, preferred_element_type=jnp.float32
    )
    return lax.all_gather(result_share, "rep", axis=0, tiled=True)


def solution(mesh):
    return jax.shard_map(
        per_device,
        mesh=mesh,
        in_specs=(
            P("row", None),
            P("row", "rep", None, None),
            P("row", "rep", None),
            P("row", "rep"),
            P("row"),
            P(),
            P(),
            P(),
            P(),
        ),
        out_specs=P("row", None),
        check_vma=False,
    )
```

profile of v0, /device:TPU:8, one launch (start us, length us, event | category | flops | bytes accessed | tf_op | source)
XLA Modules:
  0.0 450.7 jit_solution(470907498952820726)
XLA Ops:
  6.5 0.7 all-gather.3.cloned.1.call-update
  7.9 0.8 fusion.24
  8.7 0.7 and_bitcast_fusion
  9.4 115.7 %all-gather.3.cloned.1.call-done = bf16[32768,128]{1,0:T(8,128)(2,1)} async-done(((bf16[512,128]{1,0:T(8,128)(2,1)}), bf16[32768,128]{1,0:T(8,128)(2,1)}) %all-gather.3.cloned.1.call-update) | async-done | bytes 8388624 | tf_op jit(solution)/shard_map/all_gather | solution.py:39
  125.0 6.4 %gather_fusion = bf16[64,256,128]{2,1,0:T(8,128)(2,1)} fusion(bf16[128,256,128]{2,1,0:T(8,128)(2,1)} %bitcast.31, s32[1024]{0:T(1024)S(1)} %pad_clamp_fusion), kind=kCustom, calls=%fused_computation | custom fusion | bytes 8388864 | tf_op jit(solution)/shard_map/jit(_take)/gather | solution.py:63
  131.5 12.6 %fusion.8 = f32[64,256,128]{1,2,0:T(8,128)} fusion(bf16[64,1,256,256]{3,2,1,0:T(8,128)(2,1)} %param.10, bf16[64,256,128]{2,1,0:T(8,128)(2,1)} %gather_fusion, pred[64]{0:T(512)(128)(4,1)S(1)} %and_bitcast_fusion), kind=kOutput, calls=%fused_computation.13 | convolution fusion | flops 1075838976 | bytes 20971584 | tf_op jit(solution)/shard_map/sij,sjf->sif/dot_general | solution.py:64
  144.0 9.0 %copy.13 = f32[64,256,128]{2,1,0:T(8,128)} copy(f32[64,256,128]{1,2,0:T(8,128)} %fusion.8) | data formatting | bytes 16777216 | tf_op jit(solution)/shard_map/sij,sjf->sif/dot_general | solution.py:64
  153.0 12.3 %scatter_fusion = f32[3,256,128]{2,1,0:T(8,128)S(1)} fusion(f32[3,256,128]{2,1,0:T(8,128)S(1)} %broadcast_in_dim.39, s32[64]{0:T(128)S(1)} %get-tuple-element.6, f32[64,256,128]{2,1,0:T(8,128)} %copy.13), kind=kCustom, calls=%fused_computation.2 | custom fusion | flops 2097152 | bytes 25166080 | tf_op jit(solution)/shard_map/scatter-add | solution.py:67
  165.3 0.7 slice.20
  166.1 3.4 all-to-all-start
  169.5 0.8 dynamic-slice_convert_fusion
  170.3 0.9 fusion.18
  171.2 7.8 %all-to-all-done = f32[4,128,128]{2,1,0:T(8,128)S(1)} async-done(((f32[4,128,128]{2,1,0:T(8,128)}), f32[4,128,128]{2,1,0:T(8,128)S(1)}, u32[]{:S(2)}, u32[]{:S(2)}) %all-to-all-start) | async-done | bytes 262176 | tf_op jit(solution)/shard_map/all_to_all | solution.py:16
  179.2 10.9 %all_to_all.15 = bf16[4,128,256]{2,1,0:T(8,128)(2,1)} all-to-all(bf16[4,128,256]{2,1,0:T(8,128)(2,1)S(1)} %broadcast_in_dim.45), channel_id=1, replica_groups=mesh['row'=64,'rep'=4] {'rep'}, dimensions={0} | all-to-all | bytes 524288 | tf_op jit(solution)/shard_map/all_to_all | solution.py:22
  190.2 148.0 %all-gather.5.cloned.1.call-done = bf16[32768,256]{1,0:T(8,128)(2,1)} async-done(((bf16[512,256]{1,0:T(8,128)(2,1)}), bf16[32768,256]{1,0:T(8,128)(2,1)}) %all-gather.5.cloned.1.call-update) | async-done | bytes 16777232 | tf_op jit(solution)/shard_map/all_gather | solution.py:39
  338.2 11.3 %gather_fusion.1 = bf16[64,256,256]{2,1,0:T(8,128)(2,1)} fusion(bf16[128,256,256]{2,1,0:T(8,128)(2,1)} %bitcast.30, s32[1024]{0:T(1024)S(1)} %pad_clamp_fusion), kind=kCustom, calls=%fused_computation.1 | custom fusion | bytes 16777472 | tf_op jit(solution)/shard_map/jit(_take)/gather | solution.py:63
  349.5 17.3 %convolution_bitcast_fusion = f32[64,256,256]{1,2,0:T(8,128)} fusion(bf16[64,1,256,256]{3,2,1,0:T(8,128)(2,1)} %param.10, bf16[64,256,256]{2,1,0:T(8,128)(2,1)} %gather_fusion.1, pred[64]{0:T(512)(128)(4,1)S(1)} %and_bitcast_fusion), kind=kOutput, calls=%fused_computation.4 | convolution fusion | flops 2151677952 | bytes 33554496 | tf_op jit(solution)/shard_map/sij,sjf->sif/dot_general | solution.py:64
  366.8 17.5 %copy.15 = f32[64,256,256]{2,1,0:T(8,128)} copy(f32[64,256,256]{1,2,0:T(8,128)} %convolution_bitcast_fusion) | data formatting | bytes 33554432 | tf_op jit(solution)/shard_map/sij,sjf->sif/dot_general | solution.py:64
  384.3 22.6 %scatter_fusion.1 = f32[3,256,256]{2,1,0:T(8,128)S(1)} fusion(f32[3,256,256]{2,1,0:T(8,128)S(1)} %broadcast_in_dim.43, s32[64]{0:T(128)S(1)} %get-tuple-element.6, f32[64,256,256]{2,1,0:T(8,128)} %copy.15), kind=kCustom, calls=%fused_computation.3 | custom fusion | flops 4194304 | bytes 50331904 | tf_op jit(solution)/shard_map/scatter-add | solution.py:67
  406.9 0.8 slice.21
  407.8 5.0 %all-to-all-start.2 = ((f32[4,128,256]{2,1,0:T(8,128)}), f32[4,128,256]{2,1,0:T(8,128)S(1)}, u32[]{:S(2)}, u32[]{:S(2)}) async-start(f32[4,128,256]{2,1,0:T(8,128)} %bitcast.12), calls=%async_computation.2 | async-start | bytes 1048576 | tf_op jit(solution)/shard_map/all_to_all | solution.py:16
  412.9 14.8 %all-to-all-done.2 = f32[4,128,256]{2,1,0:T(8,128)S(1)} async-done(((f32[4,128,256]{2,1,0:T(8,128)}), f32[4,128,256]{2,1,0:T(8,128)S(1)}, u32[]{:S(2)}, u32[]{:S(2)}) %all-to-all-start.2) | async-done | bytes 524320 | tf_op jit(solution)/shard_map/all_to_all | solution.py:16
  427.9 15.1 %all_gather.11 = f32[512,256]{1,0:T(8,128)S(1)} all-gather(f32[128,256]{1,0:T(8,128)S(1)} %convolution_add_fusion), channel_id=1, replica_groups=mesh['row'=64,'rep'=4] {'rep'}, dimensions={0}, use_global_device_ids=true | all-gather | bytes 655360 | tf_op jit(solution)/shard_map/all_gather | solution.py:84
  443.1 0.8 copy.22
  (20 shorter events, 0.8 us)
Async XLA Ops:
  6.5 406.2 %copy-start = (bf16[256,256]{1,0:T(8,128)(2,1)S(1)}, bf16[256,256]{1,0:T(8,128)(2,1)}, u32[]{:S(2)}) copy-start(bf16[256,256]{1,0:T(8,128)(2,1)} %param.16) | copy-start | bytes 393220
  6.5 118.5 %all-gather.3.cloned.1.call-start = ((), (), s32[]{:S(2)}) async-start(), calls=%async_computation.3 | async-start | bytes 8519680 | tf_op jit(solution)/shard_map/all_gather | solution.py:39
  153.0 17.3 %copy-start.1 = (bf16[128,256]{1,0:T(8,128)(2,1)S(1)}, bf16[128,256]{1,0:T(8,128)(2,1)}, u32[]{:S(2)}) copy-start(bf16[128,256]{1,0:T(8,128)(2,1)} %param.14) | copy-start | bytes 196612
  153.0 26.0 %copy-start.3 = (bf16[128,256]{1,0:T(8,128)(2,1)S(1)}, bf16[128,256]{1,0:T(8,128)(2,1)}, u32[]{:S(2)}) copy-start(bf16[128,256]{1,0:T(8,128)(2,1)} %param.15) | copy-start | bytes 196612
  166.1 12.9 %all-to-all-start = ((f32[4,128,128]{2,1,0:T(8,128)}), f32[4,128,128]{2,1,0:T(8,128)S(1)}, u32[]{:S(2)}, u32[]{:S(2)}) async-start(f32[4,128,128]{2,1,0:T(8,128)} %bitcast.8), calls=%async_computation | async-start | bytes 524288 | tf_op jit(solution)/shard_map/all_to_all | solution.py:16
  169.5 168.7 %all-gather.5.cloned.1.call-start = ((), (), s32[]{:S(2)}) async-start(), calls=%async_computation.4 | async-start | bytes 17039360 | tf_op jit(solution)/shard_map/all_gather | solution.py:39
  384.3 43.4 %copy-start.2 = (bf16[256,256]{1,0:T(8,128)(2,1)S(1)}, bf16[256,256]{1,0:T(8,128)(2,1)}, u32[]{:S(2)}) copy-start(bf16[256,256]{1,0:T(8,128)(2,1)} %param.17) | copy-start | bytes 393220
  407.8 19.9 %all-to-all-start.2 = ((f32[4,128,256]{2,1,0:T(8,128)}), f32[4,128,256]{2,1,0:T(8,128)S(1)}, u32[]{:S(2)}, u32[]{:S(2)}) async-start(f32[4,128,256]{2,1,0:T(8,128)} %bitcast.12), calls=%async_computation.2 | async-start | bytes 1048576 | tf_op jit(solution)/shard_map/all_to_all | solution.py:16
Sparse Core Ops, SparseCore 0:
  10.9 114.0 all-gather.2
  190.3 147.8 all-gather.4
where the time goes:
time: 452 us; the launch traced here: 451 us
  waiting for transfers between devices  287 us (63%)
  local copies, waits for them, and re-layouts  46.6 us (10%)
  other arithmetic  37.2 us (8%)
  matrix products  31.3 us (7%)
  blocking collectives  26 us (6%)
  between operations  14.2 us (3%)
  starting transfers between devices  8.46 us (2%)
    all_gather x2, waiting for transfers between devices, spread_columns(): return lax.all_gather(whole, 'row', axis=0, tiled=True)  264 us
    scatter-add x2, other arithmetic, neighbour_sum(): jax.ops.segment_sum(products, segment, num_segments=per_block + 1)  34.9 us
    dot_general x2, matrix products, neighbour_sum(): jnp.einsum('sij,sjf->sif', tile_block, columns, preferred_element_type=jn...  29.8 us
    dot_general x2, local copies, waits for them, and re-layouts, neighbour_sum(): jnp.einsum('sij,sjf->sif', tile_block, columns, preferred_element_type=jn...  26.4 us
    all_to_all x2, waiting for transfers between devices, summed_on_arrival(): lax.all_to_all(cut_along(value, dim, peers), axis, 0, 0, tiled=True)  22.5 us
    gather x2, local copies, waits for them, and re-layouts, neighbour_sum(): columns = jnp.take(blocks, column_ids, axis=0)  17.7 us
    all_gather x1, blocking collectives, per_device(): return lax.all_gather(result_share, 'rep', axis=0, tiled=True)  15.1 us
    all_to_all x1, blocking collectives, sent_to_all(): lax.all_to_all(jnp.broadcast_to(value[None], (peers, *value.shape)), axis...  10.9 us
  transfers between devices with their start and end apart: 4, of which 4 were waited for; matrix products, arithmetic and copies ran while one was open for 1% of the time, Pallas kernels for 0%

commit v1 on v0

v1 whole, which is shorter than its diff:
```python
import jax
import jax.numpy as jnp
from jax import lax
from jax.experimental import pallas as pl
from jax.experimental.pallas import tpu as pltpu
from jax.sharding import Mesh
from jax.sharding import PartitionSpec as P

TILE = 256
SLOTS = 64
UNROLL = 4
NODES = 32768
MIB = 1 << 20


ROW = ("zh", "x", "y", "c")
PLANE = ("x", "y", "c")
ORDER = (1, 3, 2)
SWAP = [(0, 1), (1, 0)]


def shift(size, k):
    return [(i, (i + k) % size) for i in range(size)]


def in_plane(k, phase):
    pairs = []
    for x in range(4):
        for y in range(4):
            for c in range(2):
                along_x = (c + phase) % 2 == 0
                to_x, to_y = ((x + k) % 4, y) if along_x else (x, (y + k) % 4)
                pairs.append(((x * 4 + y) * 2 + c, (to_x * 4 + to_y) * 2 + c))
    return pairs


def hops(value, phase):
    return [lax.ppermute(value, PLANE, in_plane(k, phase)) for k in ORDER]


def spread(block, *extras):
    other = lax.ppermute(block, "zh", SWAP)
    other, *extras = lax.optimization_barrier((other, *extras))
    line = jnp.concatenate([block, *hops(block, 0)])
    own = jnp.concatenate([line, *hops(line, 1)])
    line = jnp.concatenate([other, *hops(other, 0)])
    one, three, two = hops(line, 1)
    near = jnp.concatenate([line, one, three])
    own_swapped = lax.ppermute(own, "c", SWAP)
    near_swapped = lax.ppermute(near, "c", SWAP)
    two_swapped = lax.ppermute(two, "c", SWAP)
    return [own, near, two, own_swapped, near_swapped, two_swapped], *extras


def plan_kernel(where, count, tiles, listed, groups, held, sem):
    load = pltpu.make_async_copy(tiles, held, sem)
    load.start()
    my_zh, my_core = lax.axis_index("zh"), lax.axis_index("c")
    my_x, my_y = lax.axis_index("x"), lax.axis_index("y")

    def step(s, carry):
        segment, column = where[0, s], where[1, s]
        core = (column >> 1) & 1
        dy = (my_y - (column >> 2)) & 3
        dx = (my_x - (column >> 4)) & 3
        dy = dy ^ (dy >> 1)
        dx = dx ^ (dx >> 1)
        outer = jnp.where(core == 0, dy, dx)
        inner = jnp.where(core == 0, dx, dy)
        part = (core ^ my_core) * 2 + ((column >> 6) ^ my_zh)
        place = part * 32 + outer * 8 + inner * 2 + (column & 1)
        segment = jnp.where(s < count[0, 0], segment, 2)
        listed[s] = segment + place * 256
        return carry

    lax.fori_loop(0, SLOTS, step, 0)
    groups[0] = (count[0, 0] + UNROLL - 1) >> 2
    load.wait()


def gather_pieces(pieces, whole):
    base = 0
    for piece in pieces:

        def move(j, carry, base=base, piece=piece):
            source = pl.ds(pl.multiple_of(j * TILE, TILE), TILE)
            target = pl.ds(pl.multiple_of(base + j * TILE, TILE), TILE)
            whole[target, :] = piece[source, :]
            return carry

        lax.fori_loop(0, piece.shape[0] // TILE, move, 0)
        base += piece.shape[0]


def tile_rows(index):
    return pl.ds(pl.multiple_of(index * TILE, TILE), TILE)


def write_quarters(total, outs):
    me = lax.axis_index("zl")
    for k, out in enumerate(outs):
        start = pl.multiple_of(((me + k) & 3) * 128, 128)
        out[...] = total[pl.ds(start, 128), :].astype(out.dtype)


def first_kernel(listed, groups, tiles, *refs):
    pieces, quarters, (whole, total) = refs[:6], refs[6:10], refs[10:]
    gather_pieces(pieces, whole)
    total[...] = jnp.zeros_like(total)

    def step(g, carry):
        products = []
        for u in range(UNROLL):
            block = whole[tile_rows(listed[g * UNROLL + u] >> 8), :]
            tile = tiles[g * UNROLL + u]
            products.append(jnp.dot(tile, block, preferred_element_type=jnp.float32))
        for u in range(UNROLL):
            total[tile_rows(listed[g * UNROLL + u] & 255), :] += products[u]
        return carry

    lax.fori_loop(0, groups[0], step, 0)
    write_quarters(total, quarters)


def second_kernel(listed, groups, tiles, features, weights, *refs):
    pieces, quarters, (whole, total) = refs[:6], refs[6:10], refs[10:]
    gather_pieces(pieces, whole)
    total[...] = jnp.zeros_like(total)

    def step(g, carry):
        for u in range(UNROLL):
            rows = tile_rows(listed[g * UNROLL + u] >> 8)
            both = jnp.concatenate([features[rows, :], whole[rows, :]], axis=1)
            hidden = jnp.dot(both, weights[...], preferred_element_type=jnp.float32)
            hidden = jnp.maximum(hidden, 0.0).astype(jnp.bfloat16)
            tile = tiles[g * UNROLL + u]
            product = jnp.dot(tile, hidden, preferred_element_type=jnp.float32)
            total[tile_rows(listed[g * UNROLL + u] & 255), :] += product
        return carry

    lax.fori_loop(0, groups[0], step, 0)
    write_quarters(total, quarters)


def arrange_kernel(*refs):
    shares, out = refs[:4], refs[4]
    me = lax.axis_index("zl")
    for k, share in enumerate(shares):
        out[pl.ds(pl.multiple_of(((me - k) & 3) * 128, 128), 128), :] = share[...]


def last_kernel(own, weights, *refs):
    shares, out = refs[:4], refs[4]
    me = lax.axis_index("zl")
    for k, share in enumerate(shares):
        rows = pl.ds(pl.multiple_of(((me - k) & 3) * 128, 128), 128)
        out[rows, :] = own[rows, :] + jnp.dot(
            share[...], weights[...], preferred_element_type=jnp.float32
        )


def space(kind):
    return pl.BlockSpec(memory_space=kind)


def call(kernel, smem, hbm, vmem, outs, kinds, scratch=(), limit=4, flops=1 << 20):
    return pl.pallas_call(
        kernel,
        out_shape=outs,
        in_specs=[space(pltpu.SMEM)] * len(smem)
        + [space(pltpu.HBM)] * len(hbm)
        + [space(pltpu.VMEM)] * len(vmem),
        out_specs=[space(kind) for kind in kinds],
        scratch_shapes=list(scratch),
        compiler_params=pltpu.CompilerParams(vmem_limit_bytes=limit * MIB),
        cost_estimate=pl.CostEstimate(flops=flops, transcendentals=0, bytes_accessed=1 << 20),
    )(*smem, *hbm, *vmem)


def quarter_shapes(width, sent):
    return [
        jax.ShapeDtypeStruct((128, width), jnp.float32 if k == 0 else sent) for k in range(4)
    ]


def over_rep(values):
    return {k: lax.ppermute(values[k], "zl", shift(4, k)) for k in ORDER}


def reduced(quarters, scale):
    total = quarters[0]
    for piece in over_rep(quarters).values():
        total = total + piece.astype(jnp.float32)
    return (total / scale).astype(jnp.bfloat16)


def shared(value):
    got = over_rep([value] * 4)
    return [value, got[1], got[2], got[3]]


def per_device(
    features, tiles, tile_where, tile_count, degree, self_one, neigh_one, self_two, neigh_two
):
    zl = lax.axis_index("zl")
    listed, groups, tiles_held = call(
        plan_kernel,
        (tile_where.reshape(SLOTS, 2).T, tile_count),
        (
            pltpu.with_memory_space_constraint(
                tiles.reshape(SLOTS, TILE, TILE), pltpu.HBM
            ),
        ),
        (),
        [
            jax.ShapeDtypeStruct((SLOTS,), jnp.int32),
            jax.ShapeDtypeStruct((1,), jnp.int32),
            pltpu.VMEM((SLOTS, TILE, TILE), jnp.bfloat16),
        ],
        [pltpu.SMEM, pltpu.SMEM, pltpu.VMEM],
        [pltpu.SemaphoreType.DMA],
        2,
    )
    scale = lax.dynamic_slice_in_dim(degree, zl * 128, 128, 0).astype(jnp.float32)[:, None]
    weights = jnp.concatenate([self_one, neigh_one])
    whole = pltpu.VMEM((NODES, 128), jnp.bfloat16)

    pieces, scale, weights = spread(features, scale, weights)
    *quarters, features_held = call(
        first_kernel,
        (listed, groups),
        (),
        (tiles_held, *pieces),
        quarter_shapes(128, jnp.float32) + [whole],
        [pltpu.VMEM] * 5,
        [pltpu.VMEM((3 * TILE, 128), jnp.float32)],
        8,
        1 << 30,
    )

    agg_one = reduced(quarters, scale)
    (own_agg,) = call(
        arrange_kernel,
        (),
        (),
        shared(agg_one),
        [jax.ShapeDtypeStruct((512, 128), jnp.bfloat16)],
        [pltpu.VMEM],
    )
    own_hidden = jnp.dot(
        jnp.concatenate([features, own_agg], axis=1), weights, preferred_element_type=jnp.float32
    )
    own_hidden = jax.nn.relu(own_hidden).astype(jnp.bfloat16)
    own_part = jnp.dot(own_hidden, self_two, preferred_element_type=jnp.float32)

    (pieces,) = spread(own_agg)
    quarters = call(
        second_kernel,
        (listed, groups),
        (),
        (tiles_held, features_held, weights, *pieces),
        quarter_shapes(256, jnp.bfloat16),
        [pltpu.VMEM] * 4,
        [whole, pltpu.VMEM((3 * TILE, 256), jnp.float32)],
        14,
        1 << 31,
    )

    (out,) = call(
        last_kernel,
        (),
        (),
        (own_part, neigh_two, *shared(reduced(quarters, scale))),
        [jax.ShapeDtypeStruct((512, 256), jnp.float32)],
        [pltpu.VMEM],
    )
    return out


def solution(mesh):
    wide = Mesh(mesh.devices.reshape(2, 4, 4, 2, 4), ("zh", "x", "y", "c", "zl"))
    return jax.shard_map(
        per_device,
        mesh=wide,
        in_specs=(
            P(ROW, None),
            P(ROW, "zl", None, None),
            P(ROW, "zl", None),
            P(ROW, "zl"),
            P(ROW),
            P(),
            P(),
            P(),
            P(),
        ),
        out_specs=P(ROW, None),
        check_vma=False,
    )
```

time: 452 us -> 171 us (0.38)
  waiting for transfers between devices: 287 us -> 71.1 us
  starting transfers between devices: 8.46 us -> 70.4 us
  local copies, waits for them, and re-layouts: 46.6 us -> 2.08 us
  other arithmetic: 37.2 us -> 1.89 us
  matrix products: 31.3 us -> 0.4 us
  blocking collectives: 26 us -> 0 us
  Pallas kernels: 0 us -> 21.9 us
  between operations: 14.2 us -> 1.06 us
    all_gather x2 -> x0, waiting for transfers between devices: 264 us -> none  [spread_columns(): return lax.all_gather(whole, 'row', axis=0, tiled=True)]
    ppermute x0 -> x44, waiting for transfers between devices: none -> 71.1 us  [the longest x24 50.7 us: hops(): return [lax.ppermute(value, PLANE, in_plane(k, phase)) for k in ORDER]]
    ppermute x0 -> x44, starting transfers between devices: none -> 70.4 us  [the longest x24 44 us: hops(): return [lax.ppermute(value, PLANE, in_plane(k, phase)) for k in ORDER]]
    scatter-add x2 -> x0, other arithmetic: 34.9 us -> none  [neighbour_sum(): jax.ops.segment_sum(products, segment, num_segments=per_block + 1)]
    dot_general x6 -> x1, matrix products: 31.3 us -> 0.4 us  [per_device(): own_part = jnp.dot(own_hidden, self_two, preferred_element_type=jnp.float32)]
    dot_general x2 -> x0, local copies, waits for them, and re-layouts: 26.4 us -> none  [neighbour_sum(): jnp.einsum('sij,sjf->sif', tile_block, columns, preferred_element_type=jn...]
    all_to_all x2 -> x0, waiting for transfers between devices: 22.5 us -> none  [summed_on_arrival(): lax.all_to_all(cut_along(value, dim, peers), axis, 0, 0, tiled=True)]
    pallas_call x0 -> x5, Pallas kernels: none -> 21.9 us  [call(): pl.pallas_call(kernel, out_shape=outs, in_specs=[space(pltpu.SMEM)] * len...]
  transfers between devices with their start and end apart: 4 -> 44, of which waited for: 4 -> 22; matrix products, arithmetic and copies ran while one was open for 1% -> 2% of each run, Pallas kernels for 0% -> 3%
where the time goes in v1:
time: 171 us; the launch traced here: 169 us
  waiting for transfers between devices  71.1 us (42%)
  starting transfers between devices  70.4 us (41%)
  Pallas kernels  21.9 us (13%)
  local copies, waits for them, and re-layouts  2.08 us (1%)
  other arithmetic  1.89 us (1%)
    ppermute x24, waiting for transfers between devices, hops(): return [lax.ppermute(value, PLANE, in_plane(k, phase)) for k in ORDER]  50.7 us
    ppermute x24, starting transfers between devices, hops(): return [lax.ppermute(value, PLANE, in_plane(k, phase)) for k in ORDER]  44 us
    pallas_call x5, Pallas kernels, call(): pl.pallas_call(kernel, out_shape=outs, in_specs=[space(pltpu.SMEM)] * len...  21.9 us
    ppermute x12, waiting for transfers between devices, over_rep(): return {k: lax.ppermute(values[k], 'zl', shift(4, k)) for k in ORDER}  17.4 us
    ppermute x12, starting transfers between devices, over_rep(): return {k: lax.ppermute(values[k], 'zl', shift(4, k)) for k in ORDER}  15.2 us
    ppermute x2, starting transfers between devices, spread(): other = lax.ppermute(block, 'zh', SWAP)  10.8 us
  transfers between devices with their start and end apart: 44, of which 22 were waited for; matrix products, arithmetic and copies ran while one was open for 2% of the time, Pallas kernels for 3%

profile of v1, /device:TPU:8, one launch (start us, length us, event | category | flops | bytes accessed | tf_op | source)
XLA Modules:
  0.0 168.8 jit_solution(3404370538342626106)
XLA Ops:
  0.0 7.2 %collective-permute-start.6 = (bf16[512,128]{1,0:T(8,128)(2,1)}, bf16[512,128]{1,0:T(8,128)(2,1)S(1)}, u32[]{:S(2)}, u32[]{:S(2)}) collective-permute-start(bf16[512,128]{1,0:T(8,128)(2,1)} %param.9), channel_id=1, source_target_pairs={{0,128},{128,0},{1,129},{129,1},{2,130},{130,2},{3,131},{131,3},{4... | collective-permute-start | bytes 393224 | tf_op jit(solution)/shard_map/ppermute | solution.py:42
  14.2 2.9 %collective-permute-done.2 = bf16[512,128]{1,0:T(8,128)(2,1)S(1)} collective-permute-done((bf16[512,128]{1,0:T(8,128)(2,1)}, bf16[512,128]{1,0:T(8,128)(2,1)S(1)}, u32[]{:S(2)}, u32[]{:S(2)}) %collective-permute-start.2) | collective-permute-done | bytes 131104 | tf_op jit(solution)/shard_map/ppermute | solution.py:38
  22.6 3.0 %collective-permute-start.8 = (bf16[512,128]{1,0:T(8,128)(2,1)S(1)}, bf16[512,128]{1,0:T(8,128)(2,1)S(1)}, u32[]{:S(2)}, u32[]{:S(2)}) collective-permute-start(bf16[512,128]{1,0:T(8,128)(2,1)S(1)} %collective-permute-done.6), channel_id=1, source_target_pairs={{0,96},{4,28},{8,104},{12,4},{16,112},{20,12},{24,120},{28,20},{32... | collective-permute-start | bytes 393224 | tf_op jit(solution)/shard_map/ppermute | solution.py:38
  27.8 6.4 %collective-permute-done.8 = bf16[512,128]{1,0:T(8,128)(2,1)S(1)} collective-permute-done((bf16[512,128]{1,0:T(8,128)(2,1)S(1)}, bf16[512,128]{1,0:T(8,128)(2,1)S(1)}, u32[]{:S(2)}, u32[]{:S(2)}) %collective-permute-start.8) | collective-permute-done | bytes 131104 | tf_op jit(solution)/shard_map/ppermute | solution.py:38
  37.7 5.9 %collective-permute-done.10 = bf16[2048,128]{1,0:T(8,128)(2,1)S(1)} collective-permute-done((bf16[2048,128]{1,0:T(8,128)(2,1)S(1)}, bf16[2048,128]{1,0:T(8,128)(2,1)S(1)}, u32[]{:S(2)}, u32[]{:S(2)}) %collective-permute-start.10) | collective-permute-done | bytes 524320 | tf_op jit(solution)/shard_map/ppermute | solution.py:38
  45.1 3.0 %collective-permute-start.12 = (bf16[2048,128]{1,0:T(8,128)(2,1)S(1)}, bf16[2048,128]{1,0:T(8,128)(2,1)S(1)}, u32[]{:S(2)}, u32[]{:S(2)}) collective-permute-start(bf16[2048,128]{1,0:T(8,128)(2,1)S(1)} %get-tuple-element.35), channel_id=1, source_target_pairs={{0,16},{4,68},{8,24},{12,76},{16,0},{20,84},{24,8},{28,92},{32,48}... | collective-permute-start | bytes 1572872 | tf_op jit(solution)/shard_map/ppermute | solution.py:38
  48.1 7.7 %collective-permute-done.12.refs_2_ = bf16[2048,128]{1,0:T(8,128)(2,1)S(1)} collective-permute-done((bf16[2048,128]{1,0:T(8,128)(2,1)S(1)}, bf16[2048,128]{1,0:T(8,128)(2,1)S(1)}, u32[]{:S(2)}, u32[]{:S(2)}) %collective-permute-start.12) | collective-permute-done | bytes 524320 | tf_op jit(solution)/shard_map/ppermute | solution.py:38
  56.5 4.5 %shard_map.91 = (s32[64]{0:T(128)S(1)}, s32[1]{0:T(128)}, bf16[64,256,256]{2,1,0:T(8,128)(2,1)S(1)}) custom-call(s32[2,64]{1,0:T(2,128)S(1)} %bitcast.9, s32[1,1]{1,0:T(1,128)S(6)} %copy.38.count, bf16[64,256,256]{2,1,0:T(8,128)(2,1)} %bitcast.10), custom_call_target="tpu_custom_call" | custom-call | flops 1048576 | bytes 1048576 | tf_op jit(solution)/shard_map/pallas_call | solution.py:167
  61.1 6.1 %shard_map.92 = (f32[128,128]{1,0:T(8,128)S(1)}, f32[128,128]{1,0:T(8,128)S(1)}, f32[128,128]{1,0:T(8,128)S(1)}, f32[128,128]{1,0:T(8,128)S(1)}, bf16[32768,128]{1,0:T(8,128)(2,1)S(1)}) custom-call(s32[64]{0:T(128)S(1)} %get-tuple-element.20.listed, s32[1]{0:T(128)} %get-tuple-element.21.groups, bf16[64,256,256]{2,1,0:T(8,128)(2,1)S(1)} %get-tuple-element.22.tiles, ...), custom_call_target="tpu_custom_call" | custom-call | flops 1073741824 | bytes 1048576 | tf_op jit(solution)/shard_map/pallas_call | solution.py:167
  68.0 3.2 %collective-permute-start.17 = (f32[128,128]{1,0:T(8,128)S(1)}, f32[128,128]{1,0:T(8,128)S(1)}, u32[]{:S(2)}, u32[]{:S(2)}) collective-permute-start(f32[128,128]{1,0:T(8,128)S(1)} %get-tuple-element.26), channel_id=1, source_target_pairs={{0,3},{1,0},{2,1},{3,2},{4,7},{5,4},{6,5},{7,6},{8,11},{9,8},{10,9... | collective-permute-start | bytes 196616 | tf_op jit(solution)/shard_map/ppermute | solution.py:187
  71.2 3.2 %collective-permute-done.18 = f32[128,128]{1,0:T(8,128)S(1)} collective-permute-done((f32[128,128]{1,0:T(8,128)S(1)}, f32[128,128]{1,0:T(8,128)S(1)}, u32[]{:S(2)}, u32[]{:S(2)}) %collective-permute-start.18) | collective-permute-done | bytes 65568 | tf_op jit(solution)/shard_map/ppermute | solution.py:187
  74.4 2.8 %collective-permute-done.16 = f32[128,128]{1,0:T(8,128)S(1)} collective-permute-done((f32[128,128]{1,0:T(8,128)S(1)}, f32[128,128]{1,0:T(8,128)S(1)}, u32[]{:S(2)}, u32[]{:S(2)}) %collective-permute-start.16) | collective-permute-done | bytes 65568 | tf_op jit(solution)/shard_map/ppermute | solution.py:187
  78.7 2.6 %collective-permute-start.21 = (bf16[128,128]{1,0:T(8,128)(2,1)S(1)}, bf16[128,128]{1,0:T(8,128)(2,1)S(1)}, u32[]{:S(2)}, u32[]{:S(2)}) collective-permute-start(bf16[128,128]{1,0:T(8,128)(2,1)S(1)} %divide_convert_fusion.1.refs_0_), channel_id=1, source_target_pairs={{0,3},{1,0},{2,1},{3,2},{4,7},{5,4},{6,5},{7,6},{8,11},{9,8},{10,9... | collective-permute-start | bytes 98312 | tf_op jit(solution)/shard_map/ppermute | solution.py:187
  87.9 3.6 %collective-permute-start.28 = (bf16[512,128]{1,0:T(8,128)(2,1)S(1)}, bf16[512,128]{1,0:T(8,128)(2,1)S(1)}, u32[]{:S(2)}, u32[]{:S(2)}) collective-permute-start(bf16[512,128]{1,0:T(8,128)(2,1)S(1)} %shard_map.93), channel_id=1, source_target_pairs={{0,128},{128,0},{1,129},{129,1},{2,130},{130,2},{3,131},{131,3},{4... | collective-permute-start | bytes 393224 | tf_op jit(solution)/shard_map/ppermute | solution.py:42
  96.9 2.8 %collective-permute-start.29 = (bf16[512,128]{1,0:T(8,128)(2,1)S(1)}, bf16[512,128]{1,0:T(8,128)(2,1)S(1)}, u32[]{:S(2)}, u32[]{:S(2)}) collective-permute-start(bf16[512,128]{1,0:T(8,128)(2,1)S(1)} %collective-permute-done.28), channel_id=1, source_target_pairs={{0,32},{4,12},{8,40},{12,20},{16,48},{20,28},{24,56},{28,4},{32,64... | collective-permute-start | bytes 393224 | tf_op jit(solution)/shard_map/ppermute | solution.py:38
  104.1 8.5 %collective-permute-start.27 = (bf16[2048,128]{1,0:T(8,128)(2,1)S(1)}, bf16[2048,128]{1,0:T(8,128)(2,1)S(1)}, u32[]{:S(2)}, u32[]{:S(2)}) collective-permute-start(bf16[2048,128]{1,0:T(8,128)(2,1)S(1)} %pad_maximum_fusion), channel_id=1, source_target_pairs={{0,16},{4,68},{8,24},{12,76},{16,0},{20,84},{24,8},{28,92},{32,48}... | collective-permute-start | bytes 1572872 | tf_op jit(solution)/shard_map/ppermute | solution.py:38
  115.7 4.2 %collective-permute-done.27 = bf16[2048,128]{1,0:T(8,128)(2,1)S(1)} collective-permute-done((bf16[2048,128]{1,0:T(8,128)(2,1)S(1)}, bf16[2048,128]{1,0:T(8,128)(2,1)S(1)}, u32[]{:S(2)}, u32[]{:S(2)}) %collective-permute-start.27) | collective-permute-done | bytes 524320 | tf_op jit(solution)/shard_map/ppermute | solution.py:38
  120.1 7.8 %collective-permute-done.32 = bf16[2048,128]{1,0:T(8,128)(2,1)S(1)} collective-permute-done((bf16[2048,128]{1,0:T(8,128)(2,1)S(1)}, bf16[2048,128]{1,0:T(8,128)(2,1)S(1)}, u32[]{:S(2)}, u32[]{:S(2)}) %collective-permute-start.32) | collective-permute-done | bytes 524320 | tf_op jit(solution)/shard_map/ppermute | solution.py:38
  129.2 9.7 %collective-permute-done.34.refs_2_ = bf16[2048,128]{1,0:T(8,128)(2,1)S(1)} collective-permute-done((bf16[2048,128]{1,0:T(8,128)(2,1)S(1)}, bf16[2048,128]{1,0:T(8,128)(2,1)S(1)}, u32[]{:S(2)}, u32[]{:S(2)}) %collective-permute-start.34) | collective-permute-done | bytes 524320 | tf_op jit(solution)/shard_map/ppermute | solution.py:38
  140.9 10.2 %shard_map.94 = (f32[128,256]{1,0:T(8,128)S(1)}, bf16[128,256]{1,0:T(8,128)(2,1)S(1)}, bf16[128,256]{1,0:T(8,128)(2,1)S(1)}, bf16[128,256]{1,0:T(8,128)(2,1)S(1)}) custom-call(s32[64]{0:T(128)S(1)} %get-tuple-element.20.listed, s32[1]{0:T(128)} %get-tuple-element.21.groups, bf16[64,256,256]{2,1,0:T(8,128)(2,1)S(1)} %get-tuple-element.22.tiles, ...), custom_call_target="tpu_custom_call" | custom-call | flops 2147483648 | bytes 1048576 | tf_op jit(solution)/shard_map/pallas_call | solution.py:167
  151.2 3.2 %collective-permute-start.39 = (bf16[128,256]{1,0:T(8,128)(2,1)S(1)}, bf16[128,256]{1,0:T(8,128)(2,1)S(1)}, u32[]{:S(2)}, u32[]{:S(2)}) collective-permute-start(bf16[128,256]{1,0:T(8,128)(2,1)S(1)} %get-tuple-element.33), channel_id=1, source_target_pairs={{0,3},{1,0},{2,1},{3,2},{4,7},{5,4},{6,5},{7,6},{8,11},{9,8},{10,9... | collective-permute-start | bytes 196616 | tf_op jit(solution)/shard_map/ppermute | solution.py:187
  154.5 3.0 %collective-permute-done.40 = bf16[128,256]{1,0:T(8,128)(2,1)S(1)} collective-permute-done((bf16[128,256]{1,0:T(8,128)(2,1)S(1)}, bf16[128,256]{1,0:T(8,128)(2,1)S(1)}, u32[]{:S(2)}, u32[]{:S(2)}) %collective-permute-start.40) | collective-permute-done | bytes 65568 | tf_op jit(solution)/shard_map/ppermute | solution.py:187
  157.4 3.1 %collective-permute-done.38 = bf16[128,256]{1,0:T(8,128)(2,1)S(1)} collective-permute-done((bf16[128,256]{1,0:T(8,128)(2,1)S(1)}, bf16[128,256]{1,0:T(8,128)(2,1)S(1)}, u32[]{:S(2)}, u32[]{:S(2)}) %collective-permute-start.38) | collective-permute-done | bytes 65568 | tf_op jit(solution)/shard_map/ppermute | solution.py:187
  161.6 2.9 %collective-permute-start.43 = (bf16[128,256]{1,0:T(8,128)(2,1)S(1)}, bf16[128,256]{1,0:T(8,128)(2,1)S(1)}, u32[]{:S(2)}, u32[]{:S(2)}) collective-permute-start(bf16[128,256]{1,0:T(8,128)(2,1)S(1)} %divide_convert_fusion.refs_0_), channel_id=1, source_target_pairs={{0,3},{1,0},{2,1},{3,2},{4,7},{5,4},{6,5},{7,6},{8,11},{9,8},{10,9... | collective-permute-start | bytes 196616 | tf_op jit(solution)/shard_map/ppermute | solution.py:187
  (110 shorter events, 50.1 us)
Async XLA Ops:
  0.0 19.6 %collective-permute-start.6 = (bf16[512,128]{1,0:T(8,128)(2,1)}, bf16[512,128]{1,0:T(8,128)(2,1)S(1)}, u32[]{:S(2)}, u32[]{:S(2)}) collective-permute-start(bf16[512,128]{1,0:T(8,128)(2,1)} %param.9), channel_id=1, source_target_pairs={{0,128},{128,0},{1,129},{129,1},{2,130},{130,2},{3,131},{131,3},{4... | collective-permute-start | bytes 393224 | tf_op jit(solution)/shard_map/ppermute | solution.py:42
  17.2 19.3 %collective-permute-start.3 = (bf16[2048,128]{1,0:T(8,128)(2,1)S(1)}, bf16[2048,128]{1,0:T(8,128)(2,1)S(1)}, u32[]{:S(2)}, u32[]{:S(2)}) collective-permute-start(bf16[2048,128]{1,0:T(8,128)(2,1)S(1)} %get-tuple-element.43), channel_id=1, source_target_pairs={{0,8},{4,36},{8,16},{12,44},{16,24},{20,52},{24,0},{28,60},{32,40}... | collective-permute-start | bytes 1572872 | tf_op jit(solution)/shard_map/ppermute | solution.py:38
  19.9 16.7 %collective-permute-start.4 = (bf16[2048,128]{1,0:T(8,128)(2,1)S(1)}, bf16[2048,128]{1,0:T(8,128)(2,1)S(1)}, u32[]{:S(2)}, u32[]{:S(2)}) collective-permute-start(bf16[2048,128]{1,0:T(8,128)(2,1)S(1)} %get-tuple-element.43), channel_id=1, source_target_pairs={{0,24},{4,100},{8,0},{12,108},{16,8},{20,116},{24,16},{28,124},{32... | collective-permute-start | bytes 1572872 | tf_op jit(solution)/shard_map/ppermute | solution.py:38
  20.3 17.2 %collective-permute-start.5 = (bf16[2048,128]{1,0:T(8,128)(2,1)S(1)}, bf16[2048,128]{1,0:T(8,128)(2,1)S(1)}, u32[]{:S(2)}, u32[]{:S(2)}) collective-permute-start(bf16[2048,128]{1,0:T(8,128)(2,1)S(1)} %get-tuple-element.43), channel_id=1, source_target_pairs={{0,16},{4,68},{8,24},{12,76},{16,0},{20,84},{24,8},{28,92},{32,48}... | collective-permute-start | bytes 1572872 | tf_op jit(solution)/shard_map/ppermute | solution.py:38
  22.6 11.7 %collective-permute-start.8 = (bf16[512,128]{1,0:T(8,128)(2,1)S(1)}, bf16[512,128]{1,0:T(8,128)(2,1)S(1)}, u32[]{:S(2)}, u32[]{:S(2)}) collective-permute-start(bf16[512,128]{1,0:T(8,128)(2,1)S(1)} %collective-permute-done.6), channel_id=1, source_target_pairs={{0,96},{4,28},{8,104},{12,4},{16,112},{20,12},{24,120},{28,20},{32... | collective-permute-start | bytes 393224 | tf_op jit(solution)/shard_map/ppermute | solution.py:38
  26.2 8.1 %collective-permute-start.9 = (bf16[512,128]{1,0:T(8,128)(2,1)S(1)}, bf16[512,128]{1,0:T(8,128)(2,1)S(1)}, u32[]{:S(2)}, u32[]{:S(2)}) collective-permute-start(bf16[512,128]{1,0:T(8,128)(2,1)S(1)} %collective-permute-done.6), channel_id=1, source_target_pairs={{0,64},{4,20},{8,72},{12,28},{16,80},{20,4},{24,88},{28,12},{32,96... | collective-permute-start | bytes 393224 | tf_op jit(solution)/shard_map/ppermute | solution.py:38
  34.4 9.3 %collective-permute-start.10 = (bf16[2048,128]{1,0:T(8,128)(2,1)S(1)}, bf16[2048,128]{1,0:T(8,128)(2,1)S(1)}, u32[]{:S(2)}, u32[]{:S(2)}) collective-permute-start(bf16[2048,128]{1,0:T(8,128)(2,1)S(1)} %get-tuple-element.35), channel_id=1, source_target_pairs={{0,8},{4,36},{8,16},{12,44},{16,24},{20,52},{24,0},{28,60},{32,40}... | collective-permute-start | bytes 1572872 | tf_op jit(solution)/shard_map/ppermute | solution.py:38
  35.7 9.2 %collective-permute-start.11 = (bf16[2048,128]{1,0:T(8,128)(2,1)S(1)}, bf16[2048,128]{1,0:T(8,128)(2,1)S(1)}, u32[]{:S(2)}, u32[]{:S(2)}) collective-permute-start(bf16[2048,128]{1,0:T(8,128)(2,1)S(1)} %get-tuple-element.35), channel_id=1, source_target_pairs={{0,24},{4,100},{8,0},{12,108},{16,8},{20,116},{24,16},{28,124},{32... | collective-permute-start | bytes 1572872 | tf_op jit(solution)/shard_map/ppermute | solution.py:38
  37.6 23.5 %collective-permute-start.13 = (bf16[8192,128]{1,0:T(8,128)(2,1)S(1)}, bf16[8192,128]{1,0:T(8,128)(2,1)S(1)}, u32[]{:S(2)}, u32[]{:S(2)}) collective-permute-start(bf16[8192,128]{1,0:T(8,128)(2,1)S(1)} %constant_dynamic-update-slice_fusion.4.refs_0_), channel_id=1, source_target_pairs={{0,4},{4,0},{1,5},{5,1},{2,6},{6,2},{3,7},{7,3},{8,12},{12,8},{9,1... | collective-permute-start | bytes 6291464 | tf_op jit(solution)/shard_map/ppermute | solution.py:49
  45.0 16.1 %collective-permute-start.14 = (bf16[6144,128]{1,0:T(8,128)(2,1)S(1)}, bf16[6144,128]{1,0:T(8,128)(2,1)S(1)}, u32[]{:S(2)}, u32[]{:S(2)}) collective-permute-start(bf16[6144,128]{1,0:T(8,128)(2,1)S(1)} %constant_dynamic-update-slice_fusion.15.refs_1_), channel_id=1, source_target_pairs={{0,4},{4,0},{1,5},{5,1},{2,6},{6,2},{3,7},{7,3},{8,12},{12,8},{9,1... | collective-permute-start | bytes 4718600 | tf_op jit(solution)/shard_map/ppermute | solution.py:50
  45.1 10.8 %collective-permute-start.12 = (bf16[2048,128]{1,0:T(8,128)(2,1)S(1)}, bf16[2048,128]{1,0:T(8,128)(2,1)S(1)}, u32[]{:S(2)}, u32[]{:S(2)}) collective-permute-start(bf16[2048,128]{1,0:T(8,128)(2,1)S(1)} %get-tuple-element.35), channel_id=1, source_target_pairs={{0,16},{4,68},{8,24},{12,76},{16,0},{20,84},{24,8},{28,92},{32,48}... | collective-permute-start | bytes 1572872 | tf_op jit(solution)/shard_map/ppermute | solution.py:38
  83.7 7.8 %collective-permute-start.22 = (bf16[512,128]{1,0:T(8,128)(2,1)S(1)}, bf16[512,128]{1,0:T(8,128)(2,1)S(1)}, u32[]{:S(2)}, u32[]{:S(2)}) collective-permute-start(bf16[512,128]{1,0:T(8,128)(2,1)S(1)} %shard_map.93), channel_id=1, source_target_pairs={{0,32},{4,12},{8,40},{12,20},{16,48},{20,28},{24,56},{28,4},{32,64... | collective-permute-start | bytes 393224 | tf_op jit(solution)/shard_map/ppermute | solution.py:38
  87.9 9.0 %collective-permute-start.28 = (bf16[512,128]{1,0:T(8,128)(2,1)S(1)}, bf16[512,128]{1,0:T(8,128)(2,1)S(1)}, u32[]{:S(2)}, u32[]{:S(2)}) collective-permute-start(bf16[512,128]{1,0:T(8,128)(2,1)S(1)} %shard_map.93), channel_id=1, source_target_pairs={{0,128},{128,0},{1,129},{129,1},{2,130},{130,2},{3,131},{131,3},{4... | collective-permute-start | bytes 393224 | tf_op jit(solution)/shard_map/ppermute | solution.py:42
  93.6 22.0 %collective-permute-start.25 = (bf16[2048,128]{1,0:T(8,128)(2,1)S(1)}, bf16[2048,128]{1,0:T(8,128)(2,1)S(1)}, u32[]{:S(2)}, u32[]{:S(2)}) collective-permute-start(bf16[2048,128]{1,0:T(8,128)(2,1)S(1)} %pad_maximum_fusion), channel_id=1, source_target_pairs={{0,8},{4,36},{8,16},{12,44},{16,24},{20,52},{24,0},{28,60},{32,40}... | collective-permute-start | bytes 1572872 | tf_op jit(solution)/shard_map/ppermute | solution.py:38
  95.8 19.8 %collective-permute-start.26 = (bf16[2048,128]{1,0:T(8,128)(2,1)S(1)}, bf16[2048,128]{1,0:T(8,128)(2,1)S(1)}, u32[]{:S(2)}, u32[]{:S(2)}) collective-permute-start(bf16[2048,128]{1,0:T(8,128)(2,1)S(1)} %pad_maximum_fusion), channel_id=1, source_target_pairs={{0,24},{4,100},{8,0},{12,108},{16,8},{20,116},{24,16},{28,124},{32... | collective-permute-start | bytes 1572872 | tf_op jit(solution)/shard_map/ppermute | solution.py:38
  96.9 7.3 %collective-permute-start.29 = (bf16[512,128]{1,0:T(8,128)(2,1)S(1)}, bf16[512,128]{1,0:T(8,128)(2,1)S(1)}, u32[]{:S(2)}, u32[]{:S(2)}) collective-permute-start(bf16[512,128]{1,0:T(8,128)(2,1)S(1)} %collective-permute-done.28), channel_id=1, source_target_pairs={{0,32},{4,12},{8,40},{12,20},{16,48},{20,28},{24,56},{28,4},{32,64... | collective-permute-start | bytes 393224 | tf_op jit(solution)/shard_map/ppermute | solution.py:38
  99.7 13.0 %collective-permute-start.30 = (bf16[512,128]{1,0:T(8,128)(2,1)S(1)}, bf16[512,128]{1,0:T(8,128)(2,1)S(1)}, u32[]{:S(2)}, u32[]{:S(2)}) collective-permute-start(bf16[512,128]{1,0:T(8,128)(2,1)S(1)} %collective-permute-done.28), channel_id=1, source_target_pairs={{0,96},{4,28},{8,104},{12,4},{16,112},{20,12},{24,120},{28,20},{32... | collective-permute-start | bytes 393224 | tf_op jit(solution)/shard_map/ppermute | solution.py:38
  101.3 11.4 %collective-permute-start.31 = (bf16[512,128]{1,0:T(8,128)(2,1)S(1)}, bf16[512,128]{1,0:T(8,128)(2,1)S(1)}, u32[]{:S(2)}, u32[]{:S(2)}) collective-permute-start(bf16[512,128]{1,0:T(8,128)(2,1)S(1)} %collective-permute-done.28), channel_id=1, source_target_pairs={{0,64},{4,20},{8,72},{12,28},{16,80},{20,4},{24,88},{28,12},{32,96... | collective-permute-start | bytes 393224 | tf_op jit(solution)/shard_map/ppermute | solution.py:38
  104.1 15.8 %collective-permute-start.27 = (bf16[2048,128]{1,0:T(8,128)(2,1)S(1)}, bf16[2048,128]{1,0:T(8,128)(2,1)S(1)}, u32[]{:S(2)}, u32[]{:S(2)}) collective-permute-start(bf16[2048,128]{1,0:T(8,128)(2,1)S(1)} %pad_maximum_fusion), channel_id=1, source_target_pairs={{0,16},{4,68},{8,24},{12,76},{16,0},{20,84},{24,8},{28,92},{32,48}... | collective-permute-start | bytes 1572872 | tf_op jit(solution)/shard_map/ppermute | solution.py:38
  112.7 15.2 %collective-permute-start.32 = (bf16[2048,128]{1,0:T(8,128)(2,1)S(1)}, bf16[2048,128]{1,0:T(8,128)(2,1)S(1)}, u32[]{:S(2)}, u32[]{:S(2)}) collective-permute-start(bf16[2048,128]{1,0:T(8,128)(2,1)S(1)} %pad_maximum_fusion.1), channel_id=1, source_target_pairs={{0,8},{4,36},{8,16},{12,44},{16,24},{20,52},{24,0},{28,60},{32,40}... | collective-permute-start | bytes 1572872 | tf_op jit(solution)/shard_map/ppermute | solution.py:38
  114.3 13.6 %collective-permute-start.33 = (bf16[2048,128]{1,0:T(8,128)(2,1)S(1)}, bf16[2048,128]{1,0:T(8,128)(2,1)S(1)}, u32[]{:S(2)}, u32[]{:S(2)}) collective-permute-start(bf16[2048,128]{1,0:T(8,128)(2,1)S(1)} %pad_maximum_fusion.1), channel_id=1, source_target_pairs={{0,24},{4,100},{8,0},{12,108},{16,8},{20,116},{24,16},{28,124},{32... | collective-permute-start | bytes 1572872 | tf_op jit(solution)/shard_map/ppermute | solution.py:38
  120.0 20.9 %collective-permute-start.35 = (bf16[8192,128]{1,0:T(8,128)(2,1)S(1)}, bf16[8192,128]{1,0:T(8,128)(2,1)S(1)}, u32[]{:S(2)}, u32[]{:S(2)}) collective-permute-start(bf16[8192,128]{1,0:T(8,128)(2,1)S(1)} %constant_dynamic-update-slice_fusion.21.refs_0_), channel_id=1, source_target_pairs={{0,4},{4,0},{1,5},{5,1},{2,6},{6,2},{3,7},{7,3},{8,12},{12,8},{9,1... | collective-permute-start | bytes 6291464 | tf_op jit(solution)/shard_map/ppermute | solution.py:49
  128.0 12.8 %collective-permute-start.36 = (bf16[6144,128]{1,0:T(8,128)(2,1)S(1)}, bf16[6144,128]{1,0:T(8,128)(2,1)S(1)}, u32[]{:S(2)}, u32[]{:S(2)}) collective-permute-start(bf16[6144,128]{1,0:T(8,128)(2,1)S(1)} %constant_dynamic-update-slice_fusion.28.refs_1_), channel_id=1, source_target_pairs={{0,4},{4,0},{1,5},{5,1},{2,6},{6,2},{3,7},{7,3},{8,12},{12,8},{9,1... | collective-permute-start | bytes 4718600 | tf_op jit(solution)/shard_map/ppermute | solution.py:50
  128.1 10.8 %collective-permute-start.34 = (bf16[2048,128]{1,0:T(8,128)(2,1)S(1)}, bf16[2048,128]{1,0:T(8,128)(2,1)S(1)}, u32[]{:S(2)}, u32[]{:S(2)}) collective-permute-start(bf16[2048,128]{1,0:T(8,128)(2,1)S(1)} %pad_maximum_fusion.1), channel_id=1, source_target_pairs={{0,16},{4,68},{8,24},{12,76},{16,0},{20,84},{24,8},{28,92},{32,48}... | collective-permute-start | bytes 1572872 | tf_op jit(solution)/shard_map/ppermute | solution.py:38
  (24 other events, 355.3 us)

commit v2 on v1

--- a/solution.py
+++ b/solution.py
@@ -17,10 +17,6 @@
 PLANE = ("x", "y", "c")
 ORDER = (1, 3, 2)
 SWAP = [(0, 1), (1, 0)]
-
-
-def shift(size, k):
-    return [(i, (i + k) % size) for i in range(size)]
 
 
 def in_plane(k, phase):
@@ -34,27 +30,41 @@
     return pairs
 
 
-def hops(value, phase):
-    return [lax.ppermute(value, PLANE, in_plane(k, phase)) for k in ORDER]
-
-
-def spread(block, *extras):
+def hops(value, phase, order=ORDER):
+    received = []
+    for k in order:
+        received.append(lax.ppermute(value, PLANE, in_plane(k, phase)))
+    return received
+
+
+def onward(one, three):
+    half = one.shape[0] // 2
+    top = lax.ppermute(one[:half], PLANE, in_plane(1, 1))
+    bottom = lax.ppermute(three[half:], PLANE, in_plane(3, 1))
+    return jnp.concatenate([top, bottom])
+
+
+def spread(block):
     other = lax.ppermute(block, "zh", SWAP)
-    other, *extras = lax.optimization_barrier((other, *extras))
-    line = jnp.concatenate([block, *hops(block, 0)])
-    own = jnp.concatenate([line, *hops(line, 1)])
-    line = jnp.concatenate([other, *hops(other, 0)])
-    one, three, two = hops(line, 1)
-    near = jnp.concatenate([line, one, three])
-    own_swapped = lax.ppermute(own, "c", SWAP)
-    near_swapped = lax.ppermute(near, "c", SWAP)
-    two_swapped = lax.ppermute(two, "c", SWAP)
-    return [own, near, two, own_swapped, near_swapped, two_swapped], *extras
-
-
-def plan_kernel(where, count, tiles, listed, groups, held, sem):
+    own_line = jnp.concatenate([block, *hops(block, 0)])
+    other_line = jnp.concatenate([other, *hops(other, 0)])
+    pieces = []
+    for line in (own_line, other_line):
+        one, three = hops(line, 1, (1, 3))
+        pieces += [jnp.concatenate([line, one, three]), onward(one, three)]
+    swapped = []
+    for piece in pieces:
+        swapped.append(lax.ppermute(piece, "c", SWAP))
+    return pieces + swapped
+
+
+def load_kernel(tiles, held, sem):
     load = pltpu.make_async_copy(tiles, held, sem)
     load.start()
+    load.wait()
+
+
+def plan_kernel(where, count, degree, self_one, neigh_one, listed, groups, scale, weights):
     my_zh, my_core = lax.axis_index("zh"), lax.axis_index("c")
     my_x, my_y = lax.axis_index("x"), lax.axis_index("y")
 
@@ -75,7 +85,10 @@
 
     lax.fori_loop(0, SLOTS, step, 0)
     groups[0] = (count[0, 0] + UNROLL - 1) >> 2
-    load.wait()
+    share = degree[pl.ds(lax.axis_index("zl"), 1), :].astype(jnp.float32)
+    scale[...] = jnp.broadcast_to(share, (128, 128)).T
+    weights[pl.ds(0, 128), :] = self_one[...]
+    weights[pl.ds(128, 128), :] = neigh_one[...]
 
 
 def gather_pieces(pieces, whole):
@@ -99,12 +112,12 @@
 def write_quarters(total, outs):
     me = lax.axis_index("zl")
     for k, out in enumerate(outs):
-        start = pl.multiple_of(((me + k) & 3) * 128, 128)
+        start = pl.multiple_of((me ^ k) * 128, 128)
         out[...] = total[pl.ds(start, 128), :].astype(out.dtype)
 
 
 def first_kernel(listed, groups, tiles, *refs):
-    pieces, quarters, (whole, total) = refs[:6], refs[6:10], refs[10:]
+    pieces, quarters, (whole, total) = refs[:8], refs[8:12], refs[12:]
     gather_pieces(pieces, whole)
     total[...] = jnp.zeros_like(total)
 
@@ -123,7 +136,7 @@
 
 
 def second_kernel(listed, groups, tiles, features, weights, *refs):
-    pieces, quarters, (whole, total) = refs[:6], refs[6:10], refs[10:]
+    pieces, quarters, (whole, total) = refs[:8], refs[8:12], refs[12:]
     gather_pieces(pieces, whole)
     total[...] = jnp.zeros_like(total)
 
@@ -146,14 +159,14 @@
     shares, out = refs[:4], refs[4]
     me = lax.axis_index("zl")
     for k, share in enumerate(shares):
-        out[pl.ds(pl.multiple_of(((me - k) & 3) * 128, 128), 128), :] = share[...]
+        out[pl.ds(pl.multiple_of((me ^ k) * 128, 128), 128), :] = share[...]
 
 
 def last_kernel(own, weights, *refs):
     shares, out = refs[:4], refs[4]
     me = lax.axis_index("zl")
     for k, share in enumerate(shares):
-        rows = pl.ds(pl.multiple_of(((me - k) & 3) * 128, 128), 128)
+        rows = pl.ds(pl.multiple_of((me ^ k) * 128, 128), 128)
         out[rows, :] = own[rows, :] + jnp.dot(
             share[...], weights[...], preferred_element_type=jnp.float32
         )
@@ -184,13 +197,14 @@
 
 
 def over_rep(values):
-    return {k: lax.ppermute(values[k], "zl", shift(4, k)) for k in ORDER}
+    return {k: lax.ppermute(values[k], "zl", [(i, i ^ k) for i in range(4)]) for k in (1, 2, 3)}
 
 
 def reduced(quarters, scale):
     total = quarters[0]
     for piece in over_rep(quarters).values():
         total = total + piece.astype(jnp.float32)
+    scale = jnp.concatenate([scale] * (total.shape[1] // 128), axis=1)
     return (total / scale).astype(jnp.bfloat16)
 
 
@@ -202,30 +216,37 @@
 def per_device(
     features, tiles, tile_where, tile_count, degree, self_one, neigh_one, self_two, neigh_two
 ):
-    zl = lax.axis_index("zl")
-    listed, groups, tiles_held = call(
+    listed, groups, scale, weights = call(
         plan_kernel,
         (tile_where.reshape(SLOTS, 2).T, tile_count),
+        (),
+        (degree.reshape(4, 128), self_one, neigh_one),
+        [
+            jax.ShapeDtypeStruct((SLOTS,), jnp.int32),
+            jax.ShapeDtypeStruct((1,), jnp.int32),
+            jax.ShapeDtypeStruct((128, 128), jnp.float32),
+            jax.ShapeDtypeStruct((256, 256), jnp.bfloat16),
+        ],
+        [pltpu.SMEM, pltpu.SMEM, pltpu.VMEM, pltpu.VMEM],
+        limit=2,
+    )
+    (tiles_held,) = call(
+        load_kernel,
+        (),
         (
             pltpu.with_memory_space_constraint(
                 tiles.reshape(SLOTS, TILE, TILE), pltpu.HBM
             ),
         ),
         (),
-        [
-            jax.ShapeDtypeStruct((SLOTS,), jnp.int32),
-            jax.ShapeDtypeStruct((1,), jnp.int32),
-            pltpu.VMEM((SLOTS, TILE, TILE), jnp.bfloat16),
-        ],
-        [pltpu.SMEM, pltpu.SMEM, pltpu.VMEM],
+        [pltpu.VMEM((SLOTS, TILE, TILE), jnp.bfloat16)],
+        [pltpu.VMEM],
         [pltpu.SemaphoreType.DMA],
         2,
     )
-    scale = lax.dynamic_slice_in_dim(degree, zl * 128, 128, 0).astype(jnp.float32)[:, None]
-    weights = jnp.concatenate([self_one, neigh_one])
     whole = pltpu.VMEM((NODES, 128), jnp.bfloat16)
 
-    pieces, scale, weights = spread(features, scale, weights)
+    pieces = spread(features)
     *quarters, features_held = call(
         first_kernel,
         (listed, groups),
@@ -253,7 +274,7 @@
     own_hidden = jax.nn.relu(own_hidden).astype(jnp.bfloat16)
     own_part = jnp.dot(own_hidden, self_two, preferred_element_type=jnp.float32)
 
-    (pieces,) = spread(own_agg)
+    pieces = spread(own_agg)
     quarters = call(
         second_kernel,
         (listed, groups),

time: 171 us -> 165 us (0.965)
  waiting for transfers between devices: 71.1 us -> 64.8 us
  other arithmetic: 1.89 us -> 0.1 us
    ppermute x42 -> x48, waiting for transfers between devices: 70.1 us -> 61.1 us  [the longest x20 31.3 us: hops(): received.append(lax.ppermute(value, PLANE, in_plane(k, phase)))]
    ppermute x2, waiting for transfers between devices: 1.02 us -> 3.69 us  [spread(): other = lax.ppermute(block, 'zh', SWAP)]
    pallas_call x5 -> x6, Pallas kernels: 21.9 us -> 23.1 us  [call(): pl.pallas_call(kernel, out_shape=outs, in_specs=[space(pltpu.SMEM)] * len...]
    ppermute x42 -> x48, starting transfers between devices: 59.6 us -> 59 us  [the longest x20 27.3 us: hops(): received.append(lax.ppermute(value, PLANE, in_plane(k, phase)))]
  transfers between devices with their start and end apart: 44 -> 50, of which waited for: 22 -> 26; matrix products, arithmetic and copies ran while one was open for 2% -> 2% of each run, Pallas kernels for 3% -> 4%
where the time goes in v2:
time: 165 us; the launch traced here: 162 us
  starting transfers between devices  70.2 us (43%)
  waiting for transfers between devices  64.8 us (39%)
  Pallas kernels  23.1 us (14%)
  local copies, waits for them, and re-layouts  2.39 us (1%)
    ppermute x20, waiting for transfers between devices, hops(): received.append(lax.ppermute(value, PLANE, in_plane(k, phase)))  31.3 us
    ppermute x20, starting transfers between devices, hops(): received.append(lax.ppermute(value, PLANE, in_plane(k, phase)))  27.3 us
    pallas_call x6, Pallas kernels, call(): pl.pallas_call(kernel, out_shape=outs, in_specs=[space(pltpu.SMEM)] * len...  23.1 us
    ppermute x12, starting transfers between devices, over_rep(): lax.ppermute(values[k], 'zl', [(i, i ^ k) for i in range(4)])  17.9 us
    ppermute x12, waiting for transfers between devices, over_rep(): lax.ppermute(values[k], 'zl', [(i, i ^ k) for i in range(4)])  15.7 us
    ppermute x2, starting transfers between devices, spread(): other = lax.ppermute(block, 'zh', SWAP)  11.3 us
    ppermute x4, starting transfers between devices, onward(): top = lax.ppermute(one[:half], PLANE, in_plane(1, 1))  7.54 us
    ppermute x4, waiting for transfers between devices, onward(): bottom = lax.ppermute(three[half:], PLANE, in_plane(3, 1))  7.34 us
  transfers between devices with their start and end apart: 50, of which 26 were waited for; matrix products, arithmetic and copies ran while one was open for 2% of the time, Pallas kernels for 4%

profile of v2, /device:TPU:8, one launch (start us, length us, event | category | flops | bytes accessed | tf_op | source)
XLA Modules:
  0.0 162.2 jit_solution(5584662983341085182)
XLA Ops:
  0.0 7.2 %collective-permute-start.7 = (bf16[512,128]{1,0:T(8,128)(2,1)}, bf16[512,128]{1,0:T(8,128)(2,1)S(1)}, u32[]{:S(2)}, u32[]{:S(2)}) collective-permute-start(bf16[512,128]{1,0:T(8,128)(2,1)} %param.9), channel_id=1, source_target_pairs={{0,128},{128,0},{1,129},{129,1},{2,130},{130,2},{3,131},{131,3},{4... | collective-permute-start | bytes 393224 | tf_op jit(solution)/shard_map/ppermute | solution.py:48
  14.0 3.1 %collective-permute-done.2 = bf16[512,128]{1,0:T(8,128)(2,1)S(1)} collective-permute-done((bf16[512,128]{1,0:T(8,128)(2,1)}, bf16[512,128]{1,0:T(8,128)(2,1)S(1)}, u32[]{:S(2)}, u32[]{:S(2)}) %collective-permute-start.2) | collective-permute-done | bytes 131104 | tf_op jit(solution)/shard_map/ppermute | solution.py:36
  21.8 4.1 %collective-permute-done.9 = bf16[512,128]{1,0:T(8,128)(2,1)S(1)} collective-permute-done((bf16[512,128]{1,0:T(8,128)(2,1)S(1)}, bf16[512,128]{1,0:T(8,128)(2,1)S(1)}, u32[]{:S(2)}, u32[]{:S(2)}) %collective-permute-start.9) | collective-permute-done | bytes 131104 | tf_op jit(solution)/shard_map/ppermute | solution.py:36
  29.8 6.9 %collective-permute-done.11 = bf16[2048,128]{1,0:T(8,128)(2,1)S(1)} collective-permute-done((bf16[2048,128]{1,0:T(8,128)(2,1)S(1)}, bf16[2048,128]{1,0:T(8,128)(2,1)S(1)}, u32[]{:S(2)}, u32[]{:S(2)}) %collective-permute-start.11) | collective-permute-done | bytes 524320 | tf_op jit(solution)/shard_map/ppermute | solution.py:36
  42.7 2.2 %collective-permute-done.5 = bf16[1024,128]{1,0:T(8,128)(2,1)S(1)} collective-permute-done((bf16[1024,128]{1,0:T(8,128)(2,1)S(1)}, bf16[1024,128]{1,0:T(8,128)(2,1)S(1)}, u32[]{:S(2)}, u32[]{:S(2)}) %collective-permute-start.5) | collective-permute-done | bytes 262176 | tf_op jit(solution)/shard_map/ppermute | solution.py:42
  44.9 2.6 %collective-permute-start.14 = (bf16[1024,128]{1,0:T(8,128)(2,1)S(1)}, bf16[1024,128]{1,0:T(8,128)(2,1)S(1)}, u32[]{:S(2)}, u32[]{:S(2)}) collective-permute-start(bf16[1024,128]{1,0:T(8,128)(2,1)S(1)} %slice.35), channel_id=1, source_target_pairs={{0,24},{4,100},{8,0},{12,108},{16,8},{20,116},{24,16},{28,124},{32... | collective-permute-start | bytes 786440 | tf_op jit(solution)/shard_map/ppermute | solution.py:43
  47.8 3.7 %collective-permute-done.14 = bf16[1024,128]{1,0:T(8,128)(2,1)S(1)} collective-permute-done((bf16[1024,128]{1,0:T(8,128)(2,1)S(1)}, bf16[1024,128]{1,0:T(8,128)(2,1)S(1)}, u32[]{:S(2)}, u32[]{:S(2)}) %collective-permute-start.14) | collective-permute-done | bytes 262176 | tf_op jit(solution)/shard_map/ppermute | solution.py:43
  52.2 3.4 %shard_map.92.tiles = bf16[64,256,256]{2,1,0:T(8,128)(2,1)S(1)} custom-call(bf16[64,256,256]{2,1,0:T(8,128)(2,1)} %bitcast.9), custom_call_target="tpu_custom_call" | custom-call | flops 1048576 | bytes 1048576 | tf_op jit(solution)/shard_map/pallas_call | solution.py:180
  55.7 2.2 %shard_map.91 = (s32[64]{0:T(128)S(1)}, s32[1]{0:T(128)}, f32[128,128]{1,0:T(8,128)S(1)}, bf16[256,256]{1,0:T(8,128)(2,1)S(1)}) custom-call(s32[2,64]{1,0:T(2,128)S(1)} %bitcast.8, s32[1,1]{1,0:T(1,128)S(6)} %copy.43.count, s32[4,128]{1,0:T(4,128)S(1)} %bitcast.7, bf16[128,256]{1,0:T(8,128)(2,1)S(1)} %copy-done.2, bf16[128,256]{1,0:T(8,128)(2,1)S(1)} %copy-done.3), custom_call_target="tpu_custom_call" | custom-call | flops 1048576 | bytes 1048576 | tf_op jit(solution)/shard_map/pallas_call | solution.py:180
  58.0 6.1 %shard_map.93 = (f32[128,128]{1,0:T(8,128)S(1)}, f32[128,128]{1,0:T(8,128)S(1)}, f32[128,128]{1,0:T(8,128)S(1)}, f32[128,128]{1,0:T(8,128)S(1)}, bf16[32768,128]{1,0:T(8,128)(2,1)S(1)}) custom-call(s32[64]{0:T(128)S(1)} %get-tuple-element.18.listed, s32[1]{0:T(128)} %get-tuple-element.19.groups, bf16[64,256,256]{2,1,0:T(8,128)(2,1)S(1)} %shard_map.92.tiles, ...), custom_call_target="tpu_custom_call" | custom-call | flops 1073741824 | bytes 1048576 | tf_op jit(solution)/shard_map/pallas_call | solution.py:180
  68.6 2.3 %collective-permute-done.21 = f32[128,128]{1,0:T(8,128)S(1)} collective-permute-done((f32[128,128]{1,0:T(8,128)S(1)}, f32[128,128]{1,0:T(8,128)S(1)}, u32[]{:S(2)}, u32[]{:S(2)}) %collective-permute-start.21) | collective-permute-done | bytes 65568 | tf_op jit(solution)/shard_map/ppermute | solution.py:200
  70.9 2.8 %collective-permute-done.20 = f32[128,128]{1,0:T(8,128)S(1)} collective-permute-done((f32[128,128]{1,0:T(8,128)S(1)}, f32[128,128]{1,0:T(8,128)S(1)}, u32[]{:S(2)}, u32[]{:S(2)}) %collective-permute-start.20) | collective-permute-done | bytes 65568 | tf_op jit(solution)/shard_map/ppermute | solution.py:200
  75.5 2.7 %collective-permute-start.24 = (bf16[128,128]{1,0:T(8,128)(2,1)S(1)}, bf16[128,128]{1,0:T(8,128)(2,1)S(1)}, u32[]{:S(2)}, u32[]{:S(2)}) collective-permute-start(bf16[128,128]{1,0:T(8,128)(2,1)S(1)} %divide_convert_fusion.refs_0_), channel_id=1, source_target_pairs={{0,3},{1,2},{2,1},{3,0},{4,7},{5,6},{6,5},{7,4},{8,11},{9,10},{10,... | collective-permute-start | bytes 98312 | tf_op jit(solution)/shard_map/ppermute | solution.py:200
  79.0 2.2 %collective-permute-done.24.refs_3_ = bf16[128,128]{1,0:T(8,128)(2,1)S(1)} collective-permute-done((bf16[128,128]{1,0:T(8,128)(2,1)S(1)}, bf16[128,128]{1,0:T(8,128)(2,1)S(1)}, u32[]{:S(2)}, u32[]{:S(2)}) %collective-permute-start.24) | collective-permute-done | bytes 32800 | tf_op jit(solution)/shard_map/ppermute | solution.py:200
  81.2 2.9 %collective-permute-start.25 = (bf16[512,128]{1,0:T(8,128)(2,1)S(1)}, bf16[512,128]{1,0:T(8,128)(2,1)S(1)}, u32[]{:S(2)}, u32[]{:S(2)}) collective-permute-start(bf16[512,128]{1,0:T(8,128)(2,1)S(1)} %shard_map.94), channel_id=1, source_target_pairs={{0,32},{4,12},{8,40},{12,20},{16,48},{20,28},{24,56},{28,4},{32,64... | collective-permute-start | bytes 393224 | tf_op jit(solution)/shard_map/ppermute | solution.py:36
  86.3 4.1 %collective-permute-start.32 = (bf16[512,128]{1,0:T(8,128)(2,1)S(1)}, bf16[512,128]{1,0:T(8,128)(2,1)S(1)}, u32[]{:S(2)}, u32[]{:S(2)}) collective-permute-start(bf16[512,128]{1,0:T(8,128)(2,1)S(1)} %shard_map.94), channel_id=1, source_target_pairs={{0,128},{128,0},{1,129},{129,1},{2,130},{130,2},{3,131},{131,3},{4... | collective-permute-start | bytes 393224 | tf_op jit(solution)/shard_map/ppermute | solution.py:48
  91.0 2.4 %collective-permute-start.28 = (bf16[2048,128]{1,0:T(8,128)(2,1)S(1)}, bf16[2048,128]{1,0:T(8,128)(2,1)S(1)}, u32[]{:S(2)}, u32[]{:S(2)}) collective-permute-start(bf16[2048,128]{1,0:T(8,128)(2,1)S(1)} %pad_maximum_fusion), channel_id=1, source_target_pairs={{0,8},{4,36},{8,16},{12,44},{16,24},{20,52},{24,0},{28,60},{32,40}... | collective-permute-start | bytes 1572872 | tf_op jit(solution)/shard_map/ppermute | solution.py:36
  94.4 3.7 %collective-permute-done.32 = bf16[512,128]{1,0:T(8,128)(2,1)S(1)} collective-permute-done((bf16[512,128]{1,0:T(8,128)(2,1)S(1)}, bf16[512,128]{1,0:T(8,128)(2,1)S(1)}, u32[]{:S(2)}, u32[]{:S(2)}) %collective-permute-start.32) | collective-permute-done | bytes 131104 | tf_op jit(solution)/shard_map/ppermute | solution.py:48
  104.5 3.4 %collective-permute-done.35 = bf16[512,128]{1,0:T(8,128)(2,1)S(1)} collective-permute-done((bf16[512,128]{1,0:T(8,128)(2,1)S(1)}, bf16[512,128]{1,0:T(8,128)(2,1)S(1)}, u32[]{:S(2)}, u32[]{:S(2)}) %collective-permute-start.35) | collective-permute-done | bytes 131104 | tf_op jit(solution)/shard_map/ppermute | solution.py:36
  110.6 6.8 %collective-permute-done.36 = bf16[2048,128]{1,0:T(8,128)(2,1)S(1)} collective-permute-done((bf16[2048,128]{1,0:T(8,128)(2,1)S(1)}, bf16[2048,128]{1,0:T(8,128)(2,1)S(1)}, u32[]{:S(2)}, u32[]{:S(2)}) %collective-permute-start.36) | collective-permute-done | bytes 524320 | tf_op jit(solution)/shard_map/ppermute | solution.py:36
  128.3 3.5 %collective-permute-done.39 = bf16[1024,128]{1,0:T(8,128)(2,1)S(1)} collective-permute-done((bf16[1024,128]{1,0:T(8,128)(2,1)S(1)}, bf16[1024,128]{1,0:T(8,128)(2,1)S(1)}, u32[]{:S(2)}, u32[]{:S(2)}) %collective-permute-start.39) | collective-permute-done | bytes 262176 | tf_op jit(solution)/shard_map/ppermute | solution.py:43
  133.9 10.2 %shard_map.95 = (f32[128,256]{1,0:T(8,128)S(1)}, bf16[128,256]{1,0:T(8,128)(2,1)S(1)}, bf16[128,256]{1,0:T(8,128)(2,1)S(1)}, bf16[128,256]{1,0:T(8,128)(2,1)S(1)}) custom-call(s32[64]{0:T(128)S(1)} %get-tuple-element.18.listed, s32[1]{0:T(128)} %get-tuple-element.19.groups, bf16[64,256,256]{2,1,0:T(8,128)(2,1)S(1)} %shard_map.92.tiles, ...), custom_call_target="tpu_custom_call" | custom-call | flops 2147483648 | bytes 1048576 | tf_op jit(solution)/shard_map/pallas_call | solution.py:180
  144.7 3.9 %collective-permute-start.44 = (bf16[128,256]{1,0:T(8,128)(2,1)S(1)}, bf16[128,256]{1,0:T(8,128)(2,1)S(1)}, u32[]{:S(2)}, u32[]{:S(2)}) collective-permute-start(bf16[128,256]{1,0:T(8,128)(2,1)S(1)} %get-tuple-element.28), channel_id=1, source_target_pairs={{0,1},{1,0},{2,3},{3,2},{4,5},{5,4},{6,7},{7,6},{8,9},{9,8},{10,11... | collective-permute-start | bytes 196616 | tf_op jit(solution)/shard_map/ppermute | solution.py:200
  157.1 3.1 %collective-permute-done.48.refs_2_ = bf16[128,256]{1,0:T(8,128)(2,1)S(1)} collective-permute-done((bf16[128,256]{1,0:T(8,128)(2,1)S(1)}, bf16[128,256]{1,0:T(8,128)(2,1)S(1)}, u32[]{:S(2)}, u32[]{:S(2)}) %collective-permute-start.48) | collective-permute-done | bytes 65568 | tf_op jit(solution)/shard_map/ppermute | solution.py:200
  (140 shorter events, 65.6 us)
Async XLA Ops:
  0.0 13.2 %collective-permute-start.7 = (bf16[512,128]{1,0:T(8,128)(2,1)}, bf16[512,128]{1,0:T(8,128)(2,1)S(1)}, u32[]{:S(2)}, u32[]{:S(2)}) collective-permute-start(bf16[512,128]{1,0:T(8,128)(2,1)} %param.9), channel_id=1, source_target_pairs={{0,128},{128,0},{1,129},{129,1},{2,130},{130,2},{3,131},{131,3},{4... | collective-permute-start | bytes 393224 | tf_op jit(solution)/shard_map/ppermute | solution.py:48
  13.2 8.5 %collective-permute-start.8 = (bf16[512,128]{1,0:T(8,128)(2,1)S(1)}, bf16[512,128]{1,0:T(8,128)(2,1)S(1)}, u32[]{:S(2)}, u32[]{:S(2)}) collective-permute-start(bf16[512,128]{1,0:T(8,128)(2,1)S(1)} %collective-permute-done.7), channel_id=1, source_target_pairs={{0,32},{4,12},{8,40},{12,20},{16,48},{20,28},{24,56},{28,4},{32,64... | collective-permute-start | bytes 393224 | tf_op jit(solution)/shard_map/ppermute | solution.py:36
  17.2 12.4 %collective-permute-start.3 = (bf16[2048,128]{1,0:T(8,128)(2,1)S(1)}, bf16[2048,128]{1,0:T(8,128)(2,1)S(1)}, u32[]{:S(2)}, u32[]{:S(2)}) collective-permute-start(bf16[2048,128]{1,0:T(8,128)(2,1)S(1)} %get-tuple-element.47), channel_id=1, source_target_pairs={{0,8},{4,36},{8,16},{12,44},{16,24},{20,52},{24,0},{28,60},{32,40}... | collective-permute-start | bytes 1572872 | tf_op jit(solution)/shard_map/ppermute | solution.py:36
  18.8 10.8 %collective-permute-start.4 = (bf16[2048,128]{1,0:T(8,128)(2,1)S(1)}, bf16[2048,128]{1,0:T(8,128)(2,1)S(1)}, u32[]{:S(2)}, u32[]{:S(2)}) collective-permute-start(bf16[2048,128]{1,0:T(8,128)(2,1)S(1)} %get-tuple-element.47), channel_id=1, source_target_pairs={{0,24},{4,100},{8,0},{12,108},{16,8},{20,116},{24,16},{28,124},{32... | collective-permute-start | bytes 1572872 | tf_op jit(solution)/shard_map/ppermute | solution.py:36
  27.4 9.3 %collective-permute-start.11 = (bf16[2048,128]{1,0:T(8,128)(2,1)S(1)}, bf16[2048,128]{1,0:T(8,128)(2,1)S(1)}, u32[]{:S(2)}, u32[]{:S(2)}) collective-permute-start(bf16[2048,128]{1,0:T(8,128)(2,1)S(1)} %get-tuple-element.39), channel_id=1, source_target_pairs={{0,8},{4,36},{8,16},{12,44},{16,24},{20,52},{24,0},{28,60},{32,40}... | collective-permute-start | bytes 1572872 | tf_op jit(solution)/shard_map/ppermute | solution.py:36
  29.1 9.2 %collective-permute-start.12 = (bf16[2048,128]{1,0:T(8,128)(2,1)S(1)}, bf16[2048,128]{1,0:T(8,128)(2,1)S(1)}, u32[]{:S(2)}, u32[]{:S(2)}) collective-permute-start(bf16[2048,128]{1,0:T(8,128)(2,1)S(1)} %get-tuple-element.39), channel_id=1, source_target_pairs={{0,24},{4,100},{8,0},{12,108},{16,8},{20,116},{24,16},{28,124},{32... | collective-permute-start | bytes 1572872 | tf_op jit(solution)/shard_map/ppermute | solution.py:36
  29.7 28.3 %collective-permute-start.15 = (bf16[6144,128]{1,0:T(8,128)(2,1)S(1)}, bf16[6144,128]{1,0:T(8,128)(2,1)S(1)}, u32[]{:S(2)}, u32[]{:S(2)}) collective-permute-start(bf16[6144,128]{1,0:T(8,128)(2,1)S(1)} %constant_dynamic-update-slice_fusion.4.refs_0_), channel_id=1, source_target_pairs={{0,4},{4,0},{1,5},{5,1},{2,6},{6,2},{3,7},{7,3},{8,12},{12,8},{9,1... | collective-permute-start | bytes 4718600 | tf_op jit(solution)/shard_map/ppermute | solution.py:57
  38.3 19.7 %collective-permute-start.17 = (bf16[6144,128]{1,0:T(8,128)(2,1)S(1)}, bf16[6144,128]{1,0:T(8,128)(2,1)S(1)}, u32[]{:S(2)}, u32[]{:S(2)}) collective-permute-start(bf16[6144,128]{1,0:T(8,128)(2,1)S(1)} %constant_dynamic-update-slice_fusion.16.refs_2_), channel_id=1, source_target_pairs={{0,4},{4,0},{1,5},{5,1},{2,6},{6,2},{3,7},{7,3},{8,12},{12,8},{9,1... | collective-permute-start | bytes 4718600 | tf_op jit(solution)/shard_map/ppermute | solution.py:57
  39.9 7.7 %collective-permute-start.6 = (bf16[1024,128]{1,0:T(8,128)(2,1)S(1)}, bf16[1024,128]{1,0:T(8,128)(2,1)S(1)}, u32[]{:S(2)}, u32[]{:S(2)}) collective-permute-start(bf16[1024,128]{1,0:T(8,128)(2,1)S(1)} %slice.33), channel_id=1, source_target_pairs={{0,24},{4,100},{8,0},{12,108},{16,8},{20,116},{24,16},{28,124},{32... | collective-permute-start | bytes 786440 | tf_op jit(solution)/shard_map/ppermute | solution.py:43
  40.7 7.0 %collective-permute-start.13 = (bf16[1024,128]{1,0:T(8,128)(2,1)S(1)}, bf16[1024,128]{1,0:T(8,128)(2,1)S(1)}, u32[]{:S(2)}, u32[]{:S(2)}) collective-permute-start(bf16[1024,128]{1,0:T(8,128)(2,1)S(1)} %slice.34), channel_id=1, source_target_pairs={{0,8},{4,36},{8,16},{12,44},{16,24},{20,52},{24,0},{28,60},{32,40}... | collective-permute-start | bytes 786440 | tf_op jit(solution)/shard_map/ppermute | solution.py:42
  47.6 10.4 %collective-permute-start.16 = (bf16[2048,128]{1,0:T(8,128)(2,1)S(1)}, bf16[2048,128]{1,0:T(8,128)(2,1)S(1)}, u32[]{:S(2)}, u32[]{:S(2)}) collective-permute-start(bf16[2048,128]{1,0:T(8,128)(2,1)S(1)} %constant_dynamic-update-slice_fusion.10.refs_1_), channel_id=1, source_target_pairs={{0,4},{4,0},{1,5},{5,1},{2,6},{6,2},{3,7},{7,3},{8,12},{12,8},{9,1... | collective-permute-start | bytes 1572872 | tf_op jit(solution)/shard_map/ppermute | solution.py:57
  64.1 6.8 %collective-permute-start.21 = (f32[128,128]{1,0:T(8,128)S(1)}, f32[128,128]{1,0:T(8,128)S(1)}, u32[]{:S(2)}, u32[]{:S(2)}) collective-permute-start(f32[128,128]{1,0:T(8,128)S(1)} %get-tuple-element.23), channel_id=1, source_target_pairs={{0,3},{1,2},{2,1},{3,0},{4,7},{5,6},{6,5},{7,4},{8,11},{9,10},{10,... | collective-permute-start | bytes 196616 | tf_op jit(solution)/shard_map/ppermute | solution.py:200
  64.9 8.7 %collective-permute-start.20 = (f32[128,128]{1,0:T(8,128)S(1)}, f32[128,128]{1,0:T(8,128)S(1)}, u32[]{:S(2)}, u32[]{:S(2)}) collective-permute-start(f32[128,128]{1,0:T(8,128)S(1)} %get-tuple-element.22), channel_id=1, source_target_pairs={{0,2},{1,3},{2,0},{3,1},{4,6},{5,7},{6,4},{7,5},{8,10},{9,11},{10,... | collective-permute-start | bytes 196616 | tf_op jit(solution)/shard_map/ppermute | solution.py:200
  81.2 9.2 %collective-permute-start.25 = (bf16[512,128]{1,0:T(8,128)(2,1)S(1)}, bf16[512,128]{1,0:T(8,128)(2,1)S(1)}, u32[]{:S(2)}, u32[]{:S(2)}) collective-permute-start(bf16[512,128]{1,0:T(8,128)(2,1)S(1)} %shard_map.94), channel_id=1, source_target_pairs={{0,32},{4,12},{8,40},{12,20},{16,48},{20,28},{24,56},{28,4},{32,64... | collective-permute-start | bytes 393224 | tf_op jit(solution)/shard_map/ppermute | solution.py:36
  86.3 11.8 %collective-permute-start.32 = (bf16[512,128]{1,0:T(8,128)(2,1)S(1)}, bf16[512,128]{1,0:T(8,128)(2,1)S(1)}, u32[]{:S(2)}, u32[]{:S(2)}) collective-permute-start(bf16[512,128]{1,0:T(8,128)(2,1)S(1)} %shard_map.94), channel_id=1, source_target_pairs={{0,128},{128,0},{1,129},{129,1},{2,130},{130,2},{3,131},{131,3},{4... | collective-permute-start | bytes 393224 | tf_op jit(solution)/shard_map/ppermute | solution.py:48
  91.0 19.3 %collective-permute-start.28 = (bf16[2048,128]{1,0:T(8,128)(2,1)S(1)}, bf16[2048,128]{1,0:T(8,128)(2,1)S(1)}, u32[]{:S(2)}, u32[]{:S(2)}) collective-permute-start(bf16[2048,128]{1,0:T(8,128)(2,1)S(1)} %pad_maximum_fusion), channel_id=1, source_target_pairs={{0,8},{4,36},{8,16},{12,44},{16,24},{20,52},{24,0},{28,60},{32,40}... | collective-permute-start | bytes 1572872 | tf_op jit(solution)/shard_map/ppermute | solution.py:36
  93.4 17.0 %collective-permute-start.29 = (bf16[2048,128]{1,0:T(8,128)(2,1)S(1)}, bf16[2048,128]{1,0:T(8,128)(2,1)S(1)}, u32[]{:S(2)}, u32[]{:S(2)}) collective-permute-start(bf16[2048,128]{1,0:T(8,128)(2,1)S(1)} %pad_maximum_fusion), channel_id=1, source_target_pairs={{0,24},{4,100},{8,0},{12,108},{16,8},{20,116},{24,16},{28,124},{32... | collective-permute-start | bytes 1572872 | tf_op jit(solution)/shard_map/ppermute | solution.py:36
  107.9 9.5 %collective-permute-start.36 = (bf16[2048,128]{1,0:T(8,128)(2,1)S(1)}, bf16[2048,128]{1,0:T(8,128)(2,1)S(1)}, u32[]{:S(2)}, u32[]{:S(2)}) collective-permute-start(bf16[2048,128]{1,0:T(8,128)(2,1)S(1)} %get-tuple-element.31), channel_id=1, source_target_pairs={{0,8},{4,36},{8,16},{12,44},{16,24},{20,52},{24,0},{28,60},{32,40}... | collective-permute-start | bytes 1572872 | tf_op jit(solution)/shard_map/ppermute | solution.py:36
  109.3 9.5 %collective-permute-start.37 = (bf16[2048,128]{1,0:T(8,128)(2,1)S(1)}, bf16[2048,128]{1,0:T(8,128)(2,1)S(1)}, u32[]{:S(2)}, u32[]{:S(2)}) collective-permute-start(bf16[2048,128]{1,0:T(8,128)(2,1)S(1)} %get-tuple-element.31), channel_id=1, source_target_pairs={{0,24},{4,100},{8,0},{12,108},{16,8},{20,116},{24,16},{28,124},{32... | collective-permute-start | bytes 1572872 | tf_op jit(solution)/shard_map/ppermute | solution.py:36
  110.5 23.3 %collective-permute-start.40 = (bf16[6144,128]{1,0:T(8,128)(2,1)S(1)}, bf16[6144,128]{1,0:T(8,128)(2,1)S(1)}, u32[]{:S(2)}, u32[]{:S(2)}) collective-permute-start(bf16[6144,128]{1,0:T(8,128)(2,1)S(1)} %constant_dynamic-update-slice_fusion.24.refs_0_), channel_id=1, source_target_pairs={{0,4},{4,0},{1,5},{5,1},{2,6},{6,2},{3,7},{7,3},{8,12},{12,8},{9,1... | collective-permute-start | bytes 4718600 | tf_op jit(solution)/shard_map/ppermute | solution.py:57
  118.9 15.0 %collective-permute-start.42 = (bf16[6144,128]{1,0:T(8,128)(2,1)S(1)}, bf16[6144,128]{1,0:T(8,128)(2,1)S(1)}, u32[]{:S(2)}, u32[]{:S(2)}) collective-permute-start(bf16[6144,128]{1,0:T(8,128)(2,1)S(1)} %constant_dynamic-update-slice_fusion.36.refs_2_), channel_id=1, source_target_pairs={{0,4},{4,0},{1,5},{5,1},{2,6},{6,2},{3,7},{7,3},{8,12},{12,8},{9,1... | collective-permute-start | bytes 4718600 | tf_op jit(solution)/shard_map/ppermute | solution.py:57
  121.2 7.0 %collective-permute-start.38 = (bf16[1024,128]{1,0:T(8,128)(2,1)S(1)}, bf16[1024,128]{1,0:T(8,128)(2,1)S(1)}, u32[]{:S(2)}, u32[]{:S(2)}) collective-permute-start(bf16[1024,128]{1,0:T(8,128)(2,1)S(1)} %slice.38), channel_id=1, source_target_pairs={{0,8},{4,36},{8,16},{12,44},{16,24},{20,52},{24,0},{28,60},{32,40}... | collective-permute-start | bytes 786440 | tf_op jit(solution)/shard_map/ppermute | solution.py:42
  144.7 7.4 %collective-permute-start.44 = (bf16[128,256]{1,0:T(8,128)(2,1)S(1)}, bf16[128,256]{1,0:T(8,128)(2,1)S(1)}, u32[]{:S(2)}, u32[]{:S(2)}) collective-permute-start(bf16[128,256]{1,0:T(8,128)(2,1)S(1)} %get-tuple-element.28), channel_id=1, source_target_pairs={{0,1},{1,0},{2,3},{3,2},{4,5},{5,4},{6,7},{7,6},{8,9},{9,8},{10,11... | collective-permute-start | bytes 196616 | tf_op jit(solution)/shard_map/ppermute | solution.py:200
  153.0 7.1 %collective-permute-start.48 = (bf16[128,256]{1,0:T(8,128)(2,1)S(1)}, bf16[128,256]{1,0:T(8,128)(2,1)S(1)}, u32[]{:S(2)}, u32[]{:S(2)}) collective-permute-start(bf16[128,256]{1,0:T(8,128)(2,1)S(1)} %fusion.9.refs_0_), channel_id=1, source_target_pairs={{0,2},{1,3},{2,0},{3,1},{4,6},{5,7},{6,4},{7,5},{8,10},{9,11},{10,... | collective-permute-start | bytes 196616 | tf_op jit(solution)/shard_map/ppermute | solution.py:200
  (33 other events, 363.6 us)

commit v3 on v2

--- a/solution.py
+++ b/solution.py
@@ -9,6 +9,7 @@
 TILE = 256
 SLOTS = 64
 UNROLL = 4
+LISTED = SLOTS + UNROLL
 NODES = 32768
 MIB = 1 << 20
 
@@ -48,10 +49,11 @@
     other = lax.ppermute(block, "zh", SWAP)
     own_line = jnp.concatenate([block, *hops(block, 0)])
     other_line = jnp.concatenate([other, *hops(other, 0)])
-    pieces = []
-    for line in (own_line, other_line):
-        one, three = hops(line, 1, (1, 3))
-        pieces += [jnp.concatenate([line, one, three]), onward(one, three)]
+    one, three = hops(own_line, 1, (1, 3))
+    own_near, own_two = jnp.concatenate([own_line, one, three]), onward(one, three)
+    one, three = hops(other_line, 1, (1, 3))
+    middle = jnp.concatenate([other_line, one, three, own_two])
+    pieces = [own_near, middle, onward(one, three)]
     swapped = []
     for piece in pieces:
         swapped.append(lax.ppermute(piece, "c", SWAP))
@@ -64,11 +66,14 @@
     load.wait()
 
 
-def plan_kernel(where, count, degree, self_one, neigh_one, listed, groups, scale, weights):
+def plan_kernel(
+    where, count, degree, self_one, neigh_one, early, late, groups, scale, weights
+):
     my_zh, my_core = lax.axis_index("zh"), lax.axis_index("c")
     my_x, my_y = lax.axis_index("x"), lax.axis_index("y")
 
     def step(s, carry):
+        n_early, n_late = carry
         segment, column = where[0, s], where[1, s]
         core = (column >> 1) & 1
         dy = (my_y - (column >> 2)) & 3
@@ -77,22 +82,28 @@
         dx = dx ^ (dx >> 1)
         outer = jnp.where(core == 0, dy, dx)
         inner = jnp.where(core == 0, dx, dy)
-        part = (core ^ my_core) * 2 + ((column >> 6) ^ my_zh)
-        place = part * 32 + outer * 8 + inner * 2 + (column & 1)
-        segment = jnp.where(s < count[0, 0], segment, 2)
-        listed[s] = segment + place * 256
-        return carry
-
-    lax.fori_loop(0, SLOTS, step, 0)
-    groups[0] = (count[0, 0] + UNROLL - 1) >> 2
+        dz = (column >> 6) ^ my_zh
+        part = jnp.where(outer == 3, 48 + dz * 8, dz * 24 + outer * 8)
+        place = (core ^ my_core) * 64 + part + inner * 2 + (column & 1)
+        code = s + segment * 256 + place * 65536
+        early[n_early] = code
+        late[n_late] = code
+        is_late = jnp.where(outer == 3, 1, dz)
+        return n_early + 1 - is_late, n_late + is_late
+
+    n_early, n_late = lax.fori_loop(0, count[0, 0], step, (0, 0))
+    for u in range(UNROLL):
+        early[n_early + u] = 2 * 256
+        late[n_late + u] = 2 * 256
+    groups[0] = (n_early + UNROLL - 1) >> 2
+    groups[1] = (n_late + UNROLL - 1) >> 2
     share = degree[pl.ds(lax.axis_index("zl"), 1), :].astype(jnp.float32)
     scale[...] = jnp.broadcast_to(share, (128, 128)).T
     weights[pl.ds(0, 128), :] = self_one[...]
     weights[pl.ds(128, 128), :] = neigh_one[...]
 
 
-def gather_pieces(pieces, whole):
-    base = 0
+def gather_pieces(pieces, whole, base):
     for piece in pieces:
 
         def move(j, carry, base=base, piece=piece):
@@ -116,42 +127,56 @@
         out[...] = total[pl.ds(start, 128), :].astype(out.dtype)
 
 
-def first_kernel(listed, groups, tiles, *refs):
-    pieces, quarters, (whole, total) = refs[:8], refs[8:12], refs[12:]
-    gather_pieces(pieces, whole)
+def add_products(listed, groups, tiles, rows_of, total):
+    def step(g, carry):
+        codes = [listed[g * UNROLL + u] for u in range(UNROLL)]
+        products = [
+            jnp.dot(tiles[code & 255], rows_of(code >> 16), preferred_element_type=jnp.float32)
+            for code in codes
+        ]
+        for code, product in zip(codes, products):
+            total[tile_rows((code >> 8) & 255), :] += product
+        return carry
+
+    lax.fori_loop(0, groups, step, 0)
+
+
+def hidden_rows(features, weights, agg):
+    def rows_of(place):
+        both = jnp.concatenate([features[tile_rows(place), :], agg(place)], axis=1)
+        hidden = jnp.dot(both, weights[...], preferred_element_type=jnp.float32)
+        return jnp.maximum(hidden, 0.0).astype(jnp.bfloat16)
+
+    return rows_of
+
+
+def first_kernel(early, late, groups, tiles, *refs):
+    pieces, quarters, (whole, total) = refs[:6], refs[6:10], refs[10:]
+    gather_pieces(pieces, whole, 0)
     total[...] = jnp.zeros_like(total)
-
-    def step(g, carry):
-        products = []
-        for u in range(UNROLL):
-            block = whole[tile_rows(listed[g * UNROLL + u] >> 8), :]
-            tile = tiles[g * UNROLL + u]
-            products.append(jnp.dot(tile, block, preferred_element_type=jnp.float32))
-        for u in range(UNROLL):
-            total[tile_rows(listed[g * UNROLL + u] & 255), :] += products[u]
-        return carry
-
-    lax.fori_loop(0, groups[0], step, 0)
+    for which, listed in enumerate((early, late)):
+        add_products(
+            listed, groups[which], tiles, lambda place: whole[tile_rows(place), :], total
+        )
     write_quarters(total, quarters)
 
 
-def second_kernel(listed, groups, tiles, features, weights, *refs):
-    pieces, quarters, (whole, total) = refs[:8], refs[8:12], refs[12:]
-    gather_pieces(pieces, whole)
+def second_early(early, groups, tiles, features, weights, own, swapped, total):
+    def agg(place):
+        rows = tile_rows(place & 63)
+        return jnp.where(place >= 64, swapped[rows, :], own[rows, :])
+
     total[...] = jnp.zeros_like(total)
-
-    def step(g, carry):
-        for u in range(UNROLL):
-            rows = tile_rows(listed[g * UNROLL + u] >> 8)
-            both = jnp.concatenate([features[rows, :], whole[rows, :]], axis=1)
-            hidden = jnp.dot(both, weights[...], preferred_element_type=jnp.float32)
-            hidden = jnp.maximum(hidden, 0.0).astype(jnp.bfloat16)
-            tile = tiles[g * UNROLL + u]
-            product = jnp.dot(tile, hidden, preferred_element_type=jnp.float32)
-            total[tile_rows(listed[g * UNROLL + u] & 255), :] += product
-        return carry
-
-    lax.fori_loop(0, groups[0], step, 0)
+    add_products(early, groups[0], tiles, hidden_rows(features, weights, agg), total)
+
+
+def second_late(late, groups, tiles, features, weights, before, *refs):
+    pieces, quarters, (whole, total) = refs[:4], refs[4:8], refs[8:]
+    gather_pieces(pieces[:2], whole, 6144)
+    gather_pieces(pieces[2:], whole, NODES // 2 + 6144)
+    total[...] = before[...]
+    agg = lambda place: whole[tile_rows(place), :]
+    add_products(late, groups[1], tiles, hidden_rows(features, weights, agg), total)
     write_quarters(total, quarters)
 
 
@@ -216,18 +241,19 @@
 def per_device(
     features, tiles, tile_where, tile_count, degree, self_one, neigh_one, self_two, neigh_two
 ):
-    listed, groups, scale, weights = call(
+    early, late, groups, scale, weights = call(
         plan_kernel,
         (tile_where.reshape(SLOTS, 2).T, tile_count),
         (),
         (degree.reshape(4, 128), self_one, neigh_one),
         [
-            jax.ShapeDtypeStruct((SLOTS,), jnp.int32),
-            jax.ShapeDtypeStruct((1,), jnp.int32),
+            jax.ShapeDtypeStruct((LISTED,), jnp.int32),
+            jax.ShapeDtypeStruct((LISTED,), jnp.int32),
+            jax.ShapeDtypeStruct((2,), jnp.int32),
             jax.ShapeDtypeStruct((128, 128), jnp.float32),
             jax.ShapeDtypeStruct((256, 256), jnp.bfloat16),
         ],
-        [pltpu.SMEM, pltpu.SMEM, pltpu.VMEM, pltpu.VMEM],
+        [pltpu.SMEM] * 3 + [pltpu.VMEM] * 2,
         limit=2,
     )
     (tiles_held,) = call(
@@ -249,7 +275,7 @@
     pieces = spread(features)
     *quarters, features_held = call(
         first_kernel,
-        (listed, groups),
+        (early, late, groups),
         (),
         (tiles_held, *pieces),
         quarter_shapes(128, jnp.float32) + [whole],
@@ -275,11 +301,21 @@
     own_part = jnp.dot(own_hidden, self_two, preferred_element_type=jnp.float32)
 
     pieces = spread(own_agg)
+    (total,) = call(
+        second_early,
+        (early, groups),
+        (),
+        (tiles_held, features_held, weights, pieces[0], pieces[3]),
+        [jax.ShapeDtypeStruct((3 * TILE, 256), jnp.float32)],
+        [pltpu.VMEM],
+        limit=4,
+        flops=1 << 30,
+    )
     quarters = call(
-        second_kernel,
-        (listed, groups),
-        (),
-        (tiles_held, features_held, weights, *pieces),
+        second_late,
+        (late, groups),
+        (),
+        (tiles_held, features_held, weights, total, *pieces[1:3], *pieces[4:]),
         quarter_shapes(256, jnp.bfloat16),
         [pltpu.VMEM] * 4,
         [whole, pltpu.VMEM((3 * TILE, 256), jnp.float32)],

time: 165 us -> 158 us (0.958); the launches traced: 162 us -> 157 us
  waiting for transfers between devices: 64.8 us -> 62.2 us
    ppermute x20, waiting for transfers between devices: 31.3 us -> 24.4 us  [hops(): received.append(lax.ppermute(value, PLANE, in_plane(k, phase)))]
    ppermute x4, waiting for transfers between devices: 4.9 us -> 9.69 us  [onward(): top = lax.ppermute(one[:half], PLANE, in_plane(1, 1))]
    ppermute x4, starting transfers between devices: 7.54 us -> 4.36 us  [onward(): top = lax.ppermute(one[:half], PLANE, in_plane(1, 1))]
    ppermute x12, waiting for transfers between devices: 15.7 us -> 18.2 us  [over_rep(): lax.ppermute(values[k], 'zl', [(i, i ^ k) for i in range(4)])]
    ppermute x2, waiting for transfers between devices: 3.69 us -> 1.56 us  [spread(): other = lax.ppermute(block, 'zh', SWAP)]
    ppermute x8 -> x6, waiting for transfers between devices: 1.9 us -> 0.02 us  [spread(): swapped.append(lax.ppermute(piece, 'c', SWAP))]
    pallas_call x6 -> x7, Pallas kernels: 23.1 us -> 22 us  [call(): pl.pallas_call(kernel, out_shape=outs, in_specs=[space(pltpu.SMEM)] * len...]
  transfers between devices with their start and end apart: 50 -> 48, of which waited for: 26 -> 27; matrix products, arithmetic and copies ran while one was open for 2% -> 2% of each run, Pallas kernels for 4% -> 6%
where the time goes in v3:
time: 158 us; the launch traced here: 157 us
  starting transfers between devices  69.1 us (44%)
  waiting for transfers between devices  62.2 us (39%)
  Pallas kernels  22 us (14%)
  local copies, waits for them, and re-layouts  2.43 us (2%)
    ppermute x20, starting transfers between devices, hops(): received.append(lax.ppermute(value, PLANE, in_plane(k, phase)))  27.2 us
    ppermute x20, waiting for transfers between devices, hops(): received.append(lax.ppermute(value, PLANE, in_plane(k, phase)))  24.4 us
    pallas_call x7, Pallas kernels, call(): pl.pallas_call(kernel, out_shape=outs, in_specs=[space(pltpu.SMEM)] * len...  22 us
    ppermute x12, waiting for transfers between devices, over_rep(): lax.ppermute(values[k], 'zl', [(i, i ^ k) for i in range(4)])  18.2 us
    ppermute x12, starting transfers between devices, over_rep(): lax.ppermute(values[k], 'zl', [(i, i ^ k) for i in range(4)])  18.2 us
    ppermute x2, starting transfers between devices, spread(): other = lax.ppermute(block, 'zh', SWAP)  12.2 us
    ppermute x4, waiting for transfers between devices, onward(): top = lax.ppermute(one[:half], PLANE, in_plane(1, 1))  9.69 us
    ppermute x4, waiting for transfers between devices, onward(): bottom = lax.ppermute(three[half:], PLANE, in_plane(3, 1))  8.38 us
  transfers between devices with their start and end apart: 48, of which 27 were waited for; matrix products, arithmetic and copies ran while one was open for 2% of the time, Pallas kernels for 6%

profile of v3, /device:TPU:8, one launch (start us, length us, event | category | flops | bytes accessed | tf_op | source)
XLA Modules:
  0.0 157.4 jit_solution(1385204829854505999)
XLA Ops:
  0.0 7.2 %collective-permute-start.5 = (bf16[512,128]{1,0:T(8,128)(2,1)}, bf16[512,128]{1,0:T(8,128)(2,1)S(1)}, u32[]{:S(2)}, u32[]{:S(2)}) collective-permute-start(bf16[512,128]{1,0:T(8,128)(2,1)} %param.9), channel_id=1, source_target_pairs={{0,128},{128,0},{1,129},{129,1},{2,130},{130,2},{3,131},{131,3},{4... | collective-permute-start | bytes 393224 | tf_op jit(solution)/shard_map/ppermute | solution.py:49
  8.7 2.7 %collective-permute-start.2 = (bf16[512,128]{1,0:T(8,128)(2,1)}, bf16[512,128]{1,0:T(8,128)(2,1)S(1)}, u32[]{:S(2)}, u32[]{:S(2)}) collective-permute-start(bf16[512,128]{1,0:T(8,128)(2,1)} %param.9), channel_id=1, source_target_pairs={{0,64},{4,20},{8,72},{12,28},{16,80},{20,4},{24,88},{28,12},{32,96... | collective-permute-start | bytes 393224 | tf_op jit(solution)/shard_map/ppermute | solution.py:37
  18.8 2.3 %collective-permute-start.8 = (bf16[512,128]{1,0:T(8,128)(2,1)S(1)}, bf16[512,128]{1,0:T(8,128)(2,1)S(1)}, u32[]{:S(2)}, u32[]{:S(2)}) collective-permute-start(bf16[512,128]{1,0:T(8,128)(2,1)S(1)} %collective-permute-done.5), channel_id=1, source_target_pairs={{0,64},{4,20},{8,72},{12,28},{16,80},{20,4},{24,88},{28,12},{32,96... | collective-permute-start | bytes 393224 | tf_op jit(solution)/shard_map/ppermute | solution.py:37
  22.8 3.9 %collective-permute-done.7 = bf16[512,128]{1,0:T(8,128)(2,1)S(1)} collective-permute-done((bf16[512,128]{1,0:T(8,128)(2,1)S(1)}, bf16[512,128]{1,0:T(8,128)(2,1)S(1)}, u32[]{:S(2)}, u32[]{:S(2)}) %collective-permute-start.7) | collective-permute-done | bytes 131104 | tf_op jit(solution)/shard_map/ppermute | solution.py:37
  28.9 2.8 %collective-permute-start.12 = (bf16[1024,128]{1,0:T(8,128)(2,1)S(1)}, bf16[1024,128]{1,0:T(8,128)(2,1)S(1)}, u32[]{:S(2)}, u32[]{:S(2)}) collective-permute-start(bf16[1024,128]{1,0:T(8,128)(2,1)S(1)} %slice.33), channel_id=1, source_target_pairs={{0,24},{4,100},{8,0},{12,108},{16,8},{20,116},{24,16},{28,124},{32... | collective-permute-start | bytes 786440 | tf_op jit(solution)/shard_map/ppermute | solution.py:44
  31.8 4.2 %collective-permute-done.9 = bf16[2048,128]{1,0:T(8,128)(2,1)S(1)} collective-permute-done((bf16[2048,128]{1,0:T(8,128)(2,1)S(1)}, bf16[2048,128]{1,0:T(8,128)(2,1)S(1)}, u32[]{:S(2)}, u32[]{:S(2)}) %collective-permute-start.9) | collective-permute-done | bytes 524320 | tf_op jit(solution)/shard_map/ppermute | solution.py:37
  44.2 4.1 %collective-permute-done.13 = bf16[1024,128]{1,0:T(8,128)(2,1)S(1)} collective-permute-done((bf16[1024,128]{1,0:T(8,128)(2,1)S(1)}, bf16[1024,128]{1,0:T(8,128)(2,1)S(1)}, u32[]{:S(2)}, u32[]{:S(2)}) %collective-permute-start.13) | collective-permute-done | bytes 262176 | tf_op jit(solution)/shard_map/ppermute | solution.py:43
  48.2 2.3 %collective-permute-done.14 = bf16[1024,128]{1,0:T(8,128)(2,1)S(1)} collective-permute-done((bf16[1024,128]{1,0:T(8,128)(2,1)S(1)}, bf16[1024,128]{1,0:T(8,128)(2,1)S(1)}, u32[]{:S(2)}, u32[]{:S(2)}) %collective-permute-start.14) | collective-permute-done | bytes 262176 | tf_op jit(solution)/shard_map/ppermute | solution.py:44
  51.3 3.4 %shard_map.92.tiles = bf16[64,256,256]{2,1,0:T(8,128)(2,1)S(1)} custom-call(bf16[64,256,256]{2,1,0:T(8,128)(2,1)} %bitcast.9), custom_call_target="tpu_custom_call" | custom-call | flops 1048576 | bytes 1048576 | tf_op jit(solution)/shard_map/pallas_call | solution.py:205
  54.8 2.3 %shard_map.91 = (s32[68]{0:T(128)S(1)}, s32[68]{0:T(128)S(1)}, s32[2]{0:T(128)S(1)}, f32[128,128]{1,0:T(8,128)S(1)}, bf16[256,256]{1,0:T(8,128)(2,1)S(1)}) custom-call(s32[2,64]{1,0:T(2,128)S(1)} %bitcast.8, s32[1,1]{1,0:T(1,128)S(6)} %copy.45.count, s32[4,128]{1,0:T(4,128)S(1)} %bitcast.7, bf16[128,256]{1,0:T(8,128)(2,1)S(1)} %copy-done.2, ...), custom_call_target="tpu_custom_call" | custom-call | flops 1048576 | bytes 1048576 | tf_op jit(solution)/shard_map/pallas_call | solution.py:205
  57.2 5.4 %shard_map.93 = (f32[128,128]{1,0:T(8,128)S(1)}, f32[128,128]{1,0:T(8,128)S(1)}, f32[128,128]{1,0:T(8,128)S(1)}, f32[128,128]{1,0:T(8,128)S(1)}, bf16[32768,128]{1,0:T(8,128)(2,1)S(1)}) custom-call(s32[68]{0:T(128)S(1)} %get-tuple-element.19.early, s32[68]{0:T(128)S(1)} %get-tuple-element.20.late, s32[2]{0:T(128)S(1)} %get-tuple-element.21.groups, ...), custom_call_target="tpu_custom_call" | custom-call | flops 1073741824 | bytes 1048576 | tf_op jit(solution)/shard_map/pallas_call | solution.py:205
  64.5 2.6 %collective-permute-start.20 = (f32[128,128]{1,0:T(8,128)S(1)}, f32[128,128]{1,0:T(8,128)S(1)}, u32[]{:S(2)}, u32[]{:S(2)}) collective-permute-start(f32[128,128]{1,0:T(8,128)S(1)} %get-tuple-element.25), channel_id=1, source_target_pairs={{0,3},{1,2},{2,1},{3,0},{4,7},{5,6},{6,5},{7,4},{8,11},{9,10},{10,... | collective-permute-start | bytes 196616 | tf_op jit(solution)/shard_map/ppermute | solution.py:225
  67.2 5.0 %collective-permute-done.19 = f32[128,128]{1,0:T(8,128)S(1)} collective-permute-done((f32[128,128]{1,0:T(8,128)S(1)}, f32[128,128]{1,0:T(8,128)S(1)}, u32[]{:S(2)}, u32[]{:S(2)}) %collective-permute-start.19) | collective-permute-done | bytes 65568 | tf_op jit(solution)/shard_map/ppermute | solution.py:225
  79.7 5.0 %collective-permute-start.30 = (bf16[512,128]{1,0:T(8,128)(2,1)S(1)}, bf16[512,128]{1,0:T(8,128)(2,1)S(1)}, u32[]{:S(2)}, u32[]{:S(2)}) collective-permute-start(bf16[512,128]{1,0:T(8,128)(2,1)S(1)} %shard_map.94), channel_id=1, source_target_pairs={{0,128},{128,0},{1,129},{129,1},{2,130},{130,2},{3,131},{131,3},{4... | collective-permute-start | bytes 393224 | tf_op jit(solution)/shard_map/ppermute | solution.py:49
  90.1 2.4 %collective-permute-start.31 = (bf16[512,128]{1,0:T(8,128)(2,1)S(1)}, bf16[512,128]{1,0:T(8,128)(2,1)S(1)}, u32[]{:S(2)}, u32[]{:S(2)}) collective-permute-start(bf16[512,128]{1,0:T(8,128)(2,1)S(1)} %collective-permute-done.30), channel_id=1, source_target_pairs={{0,32},{4,12},{8,40},{12,20},{16,48},{20,28},{24,56},{28,4},{32,64... | collective-permute-start | bytes 393224 | tf_op jit(solution)/shard_map/ppermute | solution.py:37
  98.4 3.3 %collective-permute-done.32 = bf16[512,128]{1,0:T(8,128)(2,1)S(1)} collective-permute-done((bf16[512,128]{1,0:T(8,128)(2,1)S(1)}, bf16[512,128]{1,0:T(8,128)(2,1)S(1)}, u32[]{:S(2)}, u32[]{:S(2)}) %collective-permute-start.32) | collective-permute-done | bytes 131104 | tf_op jit(solution)/shard_map/ppermute | solution.py:37
  105.5 2.5 %collective-permute-start.37 = (bf16[1024,128]{1,0:T(8,128)(2,1)S(1)}, bf16[1024,128]{1,0:T(8,128)(2,1)S(1)}, u32[]{:S(2)}, u32[]{:S(2)}) collective-permute-start(bf16[1024,128]{1,0:T(8,128)(2,1)S(1)} %slice.37), channel_id=1, source_target_pairs={{0,24},{4,100},{8,0},{12,108},{16,8},{20,116},{24,16},{28,124},{32... | collective-permute-start | bytes 786440 | tf_op jit(solution)/shard_map/ppermute | solution.py:44
  108.2 4.1 %collective-permute-done.34 = bf16[2048,128]{1,0:T(8,128)(2,1)S(1)} collective-permute-done((bf16[2048,128]{1,0:T(8,128)(2,1)S(1)}, bf16[2048,128]{1,0:T(8,128)(2,1)S(1)}, u32[]{:S(2)}, u32[]{:S(2)}) %collective-permute-start.34) | collective-permute-done | bytes 524320 | tf_op jit(solution)/shard_map/ppermute | solution.py:37
  120.2 4.2 %collective-permute-done.38 = bf16[1024,128]{1,0:T(8,128)(2,1)S(1)} collective-permute-done((bf16[1024,128]{1,0:T(8,128)(2,1)S(1)}, bf16[1024,128]{1,0:T(8,128)(2,1)S(1)}, u32[]{:S(2)}, u32[]{:S(2)}) %collective-permute-start.38) | collective-permute-done | bytes 262176 | tf_op jit(solution)/shard_map/ppermute | solution.py:43
  126.7 3.7 %shard_map.95.before = f32[768,256]{1,0:T(8,128)S(1)} custom-call(s32[68]{0:T(128)S(1)} %get-tuple-element.19.early, s32[2]{0:T(128)S(1)} %get-tuple-element.21.groups, bf16[64,256,256]{2,1,0:T(8,128)(2,1)S(1)} %shard_map.92.tiles, bf16[32768,128]{1,0:T(8,128)(2,1)S(1)} %get-tuple-element.28.features, bf16[256,256]{1,0:T(8,128)(2,1)S(1)} %get-tuple-element.27.weights, ...), custom_call_target="tpu_custom_call" | custom-call | flops 1073741824 | bytes 1048576 | tf_op jit(solution)/shard_map/pallas_call | solution.py:205
  130.4 6.1 %shard_map.96 = (f32[128,256]{1,0:T(8,128)S(1)}, bf16[128,256]{1,0:T(8,128)(2,1)S(1)}, bf16[128,256]{1,0:T(8,128)(2,1)S(1)}, bf16[128,256]{1,0:T(8,128)(2,1)S(1)}) custom-call(s32[68]{0:T(128)S(1)} %get-tuple-element.20.late, s32[2]{0:T(128)S(1)} %get-tuple-element.21.groups, bf16[64,256,256]{2,1,0:T(8,128)(2,1)S(1)} %shard_map.92.tiles, ...), custom_call_target="tpu_custom_call" | custom-call | flops 2147483648 | bytes 1048576 | tf_op jit(solution)/shard_map/pallas_call | solution.py:205
  138.8 2.5 %collective-permute-start.44 = (bf16[128,256]{1,0:T(8,128)(2,1)S(1)}, bf16[128,256]{1,0:T(8,128)(2,1)S(1)}, u32[]{:S(2)}, u32[]{:S(2)}) collective-permute-start(bf16[128,256]{1,0:T(8,128)(2,1)S(1)} %get-tuple-element.32), channel_id=1, source_target_pairs={{0,3},{1,2},{2,1},{3,0},{4,7},{5,6},{6,5},{7,4},{8,11},{9,10},{10,... | collective-permute-start | bytes 196616 | tf_op jit(solution)/shard_map/ppermute | solution.py:225
  141.6 5.0 %collective-permute-done.43 = bf16[128,256]{1,0:T(8,128)(2,1)S(1)} collective-permute-done((bf16[128,256]{1,0:T(8,128)(2,1)S(1)}, bf16[128,256]{1,0:T(8,128)(2,1)S(1)}, u32[]{:S(2)}, u32[]{:S(2)}) %collective-permute-start.43) | collective-permute-done | bytes 65568 | tf_op jit(solution)/shard_map/ppermute | solution.py:225
  153.6 2.8 %collective-permute-done.46.refs_2_ = bf16[128,256]{1,0:T(8,128)(2,1)S(1)} collective-permute-done((bf16[128,256]{1,0:T(8,128)(2,1)S(1)}, bf16[128,256]{1,0:T(8,128)(2,1)S(1)}, u32[]{:S(2)}, u32[]{:S(2)}) %collective-permute-start.46) | collective-permute-done | bytes 65568 | tf_op jit(solution)/shard_map/ppermute | solution.py:225
  (137 shorter events, 66.3 us)
Async XLA Ops:
  0.0 13.8 %collective-permute-start.5 = (bf16[512,128]{1,0:T(8,128)(2,1)}, bf16[512,128]{1,0:T(8,128)(2,1)S(1)}, u32[]{:S(2)}, u32[]{:S(2)}) collective-permute-start(bf16[512,128]{1,0:T(8,128)(2,1)} %param.9), channel_id=1, source_target_pairs={{0,128},{128,0},{1,129},{129,1},{2,130},{130,2},{3,131},{131,3},{4... | collective-permute-start | bytes 393224 | tf_op jit(solution)/shard_map/ppermute | solution.py:49
  8.7 8.0 %collective-permute-start.2 = (bf16[512,128]{1,0:T(8,128)(2,1)}, bf16[512,128]{1,0:T(8,128)(2,1)S(1)}, u32[]{:S(2)}, u32[]{:S(2)}) collective-permute-start(bf16[512,128]{1,0:T(8,128)(2,1)} %param.9), channel_id=1, source_target_pairs={{0,64},{4,20},{8,72},{12,28},{16,80},{20,4},{24,88},{28,12},{32,96... | collective-permute-start | bytes 393224 | tf_op jit(solution)/shard_map/ppermute | solution.py:37
  13.8 8.9 %collective-permute-start.6 = (bf16[512,128]{1,0:T(8,128)(2,1)S(1)}, bf16[512,128]{1,0:T(8,128)(2,1)S(1)}, u32[]{:S(2)}, u32[]{:S(2)}) collective-permute-start(bf16[512,128]{1,0:T(8,128)(2,1)S(1)} %collective-permute-done.5), channel_id=1, source_target_pairs={{0,32},{4,12},{8,40},{12,20},{16,48},{20,28},{24,56},{28,4},{32,64... | collective-permute-start | bytes 393224 | tf_op jit(solution)/shard_map/ppermute | solution.py:37
  16.7 12.2 %collective-permute-start.4 = (bf16[2048,128]{1,0:T(8,128)(2,1)S(1)}, bf16[2048,128]{1,0:T(8,128)(2,1)S(1)}, u32[]{:S(2)}, u32[]{:S(2)}) collective-permute-start(bf16[2048,128]{1,0:T(8,128)(2,1)S(1)} %get-tuple-element.49), channel_id=1, source_target_pairs={{0,24},{4,100},{8,0},{12,108},{16,8},{20,116},{24,16},{28,124},{32... | collective-permute-start | bytes 1572872 | tf_op jit(solution)/shard_map/ppermute | solution.py:37
  17.2 14.5 %collective-permute-start.3 = (bf16[2048,128]{1,0:T(8,128)(2,1)S(1)}, bf16[2048,128]{1,0:T(8,128)(2,1)S(1)}, u32[]{:S(2)}, u32[]{:S(2)}) collective-permute-start(bf16[2048,128]{1,0:T(8,128)(2,1)S(1)} %get-tuple-element.49), channel_id=1, source_target_pairs={{0,8},{4,36},{8,16},{12,44},{16,24},{20,52},{24,0},{28,60},{32,40}... | collective-permute-start | bytes 1572872 | tf_op jit(solution)/shard_map/ppermute | solution.py:37
  18.8 7.9 %collective-permute-start.8 = (bf16[512,128]{1,0:T(8,128)(2,1)S(1)}, bf16[512,128]{1,0:T(8,128)(2,1)S(1)}, u32[]{:S(2)}, u32[]{:S(2)}) collective-permute-start(bf16[512,128]{1,0:T(8,128)(2,1)S(1)} %collective-permute-done.5), channel_id=1, source_target_pairs={{0,64},{4,20},{8,72},{12,28},{16,80},{20,4},{24,88},{28,12},{32,96... | collective-permute-start | bytes 393224 | tf_op jit(solution)/shard_map/ppermute | solution.py:37
  26.8 9.3 %collective-permute-start.9 = (bf16[2048,128]{1,0:T(8,128)(2,1)S(1)}, bf16[2048,128]{1,0:T(8,128)(2,1)S(1)}, u32[]{:S(2)}, u32[]{:S(2)}) collective-permute-start(bf16[2048,128]{1,0:T(8,128)(2,1)S(1)} %get-tuple-element.41), channel_id=1, source_target_pairs={{0,8},{4,36},{8,16},{12,44},{16,24},{20,52},{24,0},{28,60},{32,40}... | collective-permute-start | bytes 1572872 | tf_op jit(solution)/shard_map/ppermute | solution.py:37
  28.5 9.6 %collective-permute-start.10 = (bf16[2048,128]{1,0:T(8,128)(2,1)S(1)}, bf16[2048,128]{1,0:T(8,128)(2,1)S(1)}, u32[]{:S(2)}, u32[]{:S(2)}) collective-permute-start(bf16[2048,128]{1,0:T(8,128)(2,1)S(1)} %get-tuple-element.41), channel_id=1, source_target_pairs={{0,24},{4,100},{8,0},{12,108},{16,8},{20,116},{24,16},{28,124},{32... | collective-permute-start | bytes 1572872 | tf_op jit(solution)/shard_map/ppermute | solution.py:37
  28.9 11.9 %collective-permute-start.12 = (bf16[1024,128]{1,0:T(8,128)(2,1)S(1)}, bf16[1024,128]{1,0:T(8,128)(2,1)S(1)}, u32[]{:S(2)}, u32[]{:S(2)}) collective-permute-start(bf16[1024,128]{1,0:T(8,128)(2,1)S(1)} %slice.33), channel_id=1, source_target_pairs={{0,24},{4,100},{8,0},{12,108},{16,8},{20,116},{24,16},{28,124},{32... | collective-permute-start | bytes 786440 | tf_op jit(solution)/shard_map/ppermute | solution.py:44
  40.9 16.3 %collective-permute-start.16 = (bf16[8192,128]{1,0:T(8,128)(2,1)S(1)}, bf16[8192,128]{1,0:T(8,128)(2,1)S(1)}, u32[]{:S(2)}, u32[]{:S(2)}) collective-permute-start(bf16[8192,128]{1,0:T(8,128)(2,1)S(1)} %constant_dynamic-update-slice_fusion.14.refs_1_), channel_id=1, source_target_pairs={{0,4},{4,0},{1,5},{5,1},{2,6},{6,2},{3,7},{7,3},{8,12},{12,8},{9,1... | collective-permute-start | bytes 6291464 | tf_op jit(solution)/shard_map/ppermute | solution.py:59
  41.2 16.0 %collective-permute-start.15 = (bf16[6144,128]{1,0:T(8,128)(2,1)S(1)}, bf16[6144,128]{1,0:T(8,128)(2,1)S(1)}, u32[]{:S(2)}, u32[]{:S(2)}) collective-permute-start(bf16[6144,128]{1,0:T(8,128)(2,1)S(1)} %constant_dynamic-update-slice_fusion.4.refs_0_), channel_id=1, source_target_pairs={{0,4},{4,0},{1,5},{5,1},{2,6},{6,2},{3,7},{7,3},{8,12},{12,8},{9,1... | collective-permute-start | bytes 4718600 | tf_op jit(solution)/shard_map/ppermute | solution.py:59
  79.7 10.4 %collective-permute-start.30 = (bf16[512,128]{1,0:T(8,128)(2,1)S(1)}, bf16[512,128]{1,0:T(8,128)(2,1)S(1)}, u32[]{:S(2)}, u32[]{:S(2)}) collective-permute-start(bf16[512,128]{1,0:T(8,128)(2,1)S(1)} %shard_map.94), channel_id=1, source_target_pairs={{0,128},{128,0},{1,129},{129,1},{2,130},{130,2},{3,131},{131,3},{4... | collective-permute-start | bytes 393224 | tf_op jit(solution)/shard_map/ppermute | solution.py:49
  84.7 7.8 %collective-permute-start.26 = (bf16[512,128]{1,0:T(8,128)(2,1)S(1)}, bf16[512,128]{1,0:T(8,128)(2,1)S(1)}, u32[]{:S(2)}, u32[]{:S(2)}) collective-permute-start(bf16[512,128]{1,0:T(8,128)(2,1)S(1)} %shard_map.94), channel_id=1, source_target_pairs={{0,64},{4,20},{8,72},{12,28},{16,80},{20,4},{24,88},{28,12},{32,96... | collective-permute-start | bytes 393224 | tf_op jit(solution)/shard_map/ppermute | solution.py:37
  90.1 8.2 %collective-permute-start.31 = (bf16[512,128]{1,0:T(8,128)(2,1)S(1)}, bf16[512,128]{1,0:T(8,128)(2,1)S(1)}, u32[]{:S(2)}, u32[]{:S(2)}) collective-permute-start(bf16[512,128]{1,0:T(8,128)(2,1)S(1)} %collective-permute-done.30), channel_id=1, source_target_pairs={{0,32},{4,12},{8,40},{12,20},{16,48},{20,28},{24,56},{28,4},{32,64... | collective-permute-start | bytes 393224 | tf_op jit(solution)/shard_map/ppermute | solution.py:37
  94.2 11.2 %collective-permute-start.28 = (bf16[2048,128]{1,0:T(8,128)(2,1)S(1)}, bf16[2048,128]{1,0:T(8,128)(2,1)S(1)}, u32[]{:S(2)}, u32[]{:S(2)}) collective-permute-start(bf16[2048,128]{1,0:T(8,128)(2,1)S(1)} %pad_maximum_fusion), channel_id=1, source_target_pairs={{0,24},{4,100},{8,0},{12,108},{16,8},{20,116},{24,16},{28,124},{32... | collective-permute-start | bytes 1572872 | tf_op jit(solution)/shard_map/ppermute | solution.py:37
  94.3 13.7 %collective-permute-start.27 = (bf16[2048,128]{1,0:T(8,128)(2,1)S(1)}, bf16[2048,128]{1,0:T(8,128)(2,1)S(1)}, u32[]{:S(2)}, u32[]{:S(2)}) collective-permute-start(bf16[2048,128]{1,0:T(8,128)(2,1)S(1)} %pad_maximum_fusion), channel_id=1, source_target_pairs={{0,8},{4,36},{8,16},{12,44},{16,24},{20,52},{24,0},{28,60},{32,40}... | collective-permute-start | bytes 1572872 | tf_op jit(solution)/shard_map/ppermute | solution.py:37
  103.0 9.3 %collective-permute-start.34 = (bf16[2048,128]{1,0:T(8,128)(2,1)S(1)}, bf16[2048,128]{1,0:T(8,128)(2,1)S(1)}, u32[]{:S(2)}, u32[]{:S(2)}) collective-permute-start(bf16[2048,128]{1,0:T(8,128)(2,1)S(1)} %get-tuple-element.33), channel_id=1, source_target_pairs={{0,8},{4,36},{8,16},{12,44},{16,24},{20,52},{24,0},{28,60},{32,40}... | collective-permute-start | bytes 1572872 | tf_op jit(solution)/shard_map/ppermute | solution.py:37
  104.4 9.9 %collective-permute-start.35 = (bf16[2048,128]{1,0:T(8,128)(2,1)S(1)}, bf16[2048,128]{1,0:T(8,128)(2,1)S(1)}, u32[]{:S(2)}, u32[]{:S(2)}) collective-permute-start(bf16[2048,128]{1,0:T(8,128)(2,1)S(1)} %get-tuple-element.33), channel_id=1, source_target_pairs={{0,24},{4,100},{8,0},{12,108},{16,8},{20,116},{24,16},{28,124},{32... | collective-permute-start | bytes 1572872 | tf_op jit(solution)/shard_map/ppermute | solution.py:37
  105.5 11.6 %collective-permute-start.37 = (bf16[1024,128]{1,0:T(8,128)(2,1)S(1)}, bf16[1024,128]{1,0:T(8,128)(2,1)S(1)}, u32[]{:S(2)}, u32[]{:S(2)}) collective-permute-start(bf16[1024,128]{1,0:T(8,128)(2,1)S(1)} %slice.37), channel_id=1, source_target_pairs={{0,24},{4,100},{8,0},{12,108},{16,8},{20,116},{24,16},{28,124},{32... | collective-permute-start | bytes 786440 | tf_op jit(solution)/shard_map/ppermute | solution.py:44
  117.2 13.3 %collective-permute-start.40 = (bf16[8192,128]{1,0:T(8,128)(2,1)S(1)}, bf16[8192,128]{1,0:T(8,128)(2,1)S(1)}, u32[]{:S(2)}, u32[]{:S(2)}) collective-permute-start(bf16[8192,128]{1,0:T(8,128)(2,1)S(1)} %constant_dynamic-update-slice_fusion.34.refs_0_), channel_id=1, source_target_pairs={{0,4},{4,0},{1,5},{5,1},{2,6},{6,2},{3,7},{7,3},{8,12},{12,8},{9,1... | collective-permute-start | bytes 6291464 | tf_op jit(solution)/shard_map/ppermute | solution.py:59
  117.4 9.3 %collective-permute-start.29 = (bf16[6144,128]{1,0:T(8,128)(2,1)S(1)}, bf16[6144,128]{1,0:T(8,128)(2,1)S(1)}, u32[]{:S(2)}, u32[]{:S(2)}) collective-permute-start(bf16[6144,128]{1,0:T(8,128)(2,1)S(1)} %constant_dynamic-update-slice_fusion.24.own), channel_id=1, source_target_pairs={{0,4},{4,0},{1,5},{5,1},{2,6},{6,2},{3,7},{7,3},{8,12},{12,8},{9,1... | collective-permute-start | bytes 4718600 | tf_op jit(solution)/shard_map/ppermute | solution.py:59
  138.8 7.8 %collective-permute-start.43 = (bf16[128,256]{1,0:T(8,128)(2,1)S(1)}, bf16[128,256]{1,0:T(8,128)(2,1)S(1)}, u32[]{:S(2)}, u32[]{:S(2)}) collective-permute-start(bf16[128,256]{1,0:T(8,128)(2,1)S(1)} %get-tuple-element.31), channel_id=1, source_target_pairs={{0,2},{1,3},{2,0},{3,1},{4,6},{5,7},{6,4},{7,5},{8,10},{9,11},{10,... | collective-permute-start | bytes 196616 | tf_op jit(solution)/shard_map/ppermute | solution.py:225
  138.8 7.8 %collective-permute-start.44 = (bf16[128,256]{1,0:T(8,128)(2,1)S(1)}, bf16[128,256]{1,0:T(8,128)(2,1)S(1)}, u32[]{:S(2)}, u32[]{:S(2)}) collective-permute-start(bf16[128,256]{1,0:T(8,128)(2,1)S(1)} %get-tuple-element.32), channel_id=1, source_target_pairs={{0,3},{1,2},{2,1},{3,0},{4,7},{5,6},{6,5},{7,4},{8,11},{9,10},{10,... | collective-permute-start | bytes 196616 | tf_op jit(solution)/shard_map/ppermute | solution.py:225
  148.2 8.2 %collective-permute-start.46 = (bf16[128,256]{1,0:T(8,128)(2,1)S(1)}, bf16[128,256]{1,0:T(8,128)(2,1)S(1)}, u32[]{:S(2)}, u32[]{:S(2)}) collective-permute-start(bf16[128,256]{1,0:T(8,128)(2,1)S(1)} %fusion.9.refs_0_), channel_id=1, source_target_pairs={{0,2},{1,3},{2,0},{3,1},{4,6},{5,7},{6,4},{7,5},{8,10},{9,11},{10,... | collective-permute-start | bytes 196616 | tf_op jit(solution)/shard_map/ppermute | solution.py:225
  (31 other events, 358.1 us)

commit v4 on v3

--- a/solution.py
+++ b/solution.py
@@ -67,13 +67,13 @@
 
 
 def plan_kernel(
-    where, count, degree, self_one, neigh_one, early, late, groups, scale, weights
+    where, count, degree, self_one, neigh_one, first, second, late, groups, scale, weights
 ):
     my_zh, my_core = lax.axis_index("zh"), lax.axis_index("c")
     my_x, my_y = lax.axis_index("x"), lax.axis_index("y")
 
     def step(s, carry):
-        n_early, n_late = carry
+        n_first, n_second, n_late = carry
         segment, column = where[0, s], where[1, s]
         core = (column >> 1) & 1
         dy = (my_y - (column >> 2)) & 3
@@ -86,17 +86,18 @@
         part = jnp.where(outer == 3, 48 + dz * 8, dz * 24 + outer * 8)
         place = (core ^ my_core) * 64 + part + inner * 2 + (column & 1)
         code = s + segment * 256 + place * 65536
-        early[n_early] = code
+        first[n_first] = code
+        second[n_second] = code
         late[n_late] = code
         is_late = jnp.where(outer == 3, 1, dz)
-        return n_early + 1 - is_late, n_late + is_late
-
-    n_early, n_late = lax.fori_loop(0, count[0, 0], step, (0, 0))
-    for u in range(UNROLL):
-        early[n_early + u] = 2 * 256
-        late[n_late + u] = 2 * 256
-    groups[0] = (n_early + UNROLL - 1) >> 2
-    groups[1] = (n_late + UNROLL - 1) >> 2
+        swapped = (1 - is_late) * (core ^ my_core)
+        return n_first + 1 - is_late - swapped, n_second + swapped, n_late + is_late
+
+    counts = lax.fori_loop(0, count[0, 0], step, (0, 0, 0))
+    for i, (listed, n) in enumerate(zip((first, second, late), counts)):
+        for u in range(UNROLL):
+            listed[n + u] = 2 * 256
+        groups[i] = (n + UNROLL - 1) >> 2
     share = degree[pl.ds(lax.axis_index("zl"), 1), :].astype(jnp.float32)
     scale[...] = jnp.broadcast_to(share, (128, 128)).T
     weights[pl.ds(0, 128), :] = self_one[...]
@@ -150,24 +151,27 @@
     return rows_of
 
 
-def first_kernel(early, late, groups, tiles, *refs):
+def first_kernel(first, second, late, groups, tiles, *refs):
     pieces, quarters, (whole, total) = refs[:6], refs[6:10], refs[10:]
     gather_pieces(pieces, whole, 0)
     total[...] = jnp.zeros_like(total)
-    for which, listed in enumerate((early, late)):
+    for which, listed in enumerate((first, second, late)):
         add_products(
             listed, groups[which], tiles, lambda place: whole[tile_rows(place), :], total
         )
     write_quarters(total, quarters)
 
 
-def second_early(early, groups, tiles, features, weights, own, swapped, total):
-    def agg(place):
-        rows = tile_rows(place & 63)
-        return jnp.where(place >= 64, swapped[rows, :], own[rows, :])
-
+def second_first(listed, groups, tiles, features, weights, piece, total):
+    agg = lambda place: piece[tile_rows(place & 31), :]
     total[...] = jnp.zeros_like(total)
-    add_products(early, groups[0], tiles, hidden_rows(features, weights, agg), total)
+    add_products(listed, groups[0], tiles, hidden_rows(features, weights, agg), total)
+
+
+def second_second(listed, groups, tiles, features, weights, before, piece, total):
+    agg = lambda place: piece[tile_rows(place & 31), :]
+    total[...] = before[...]
+    add_products(listed, groups[1], tiles, hidden_rows(features, weights, agg), total)
 
 
 def second_late(late, groups, tiles, features, weights, before, *refs):
@@ -176,7 +180,7 @@
     gather_pieces(pieces[2:], whole, NODES // 2 + 6144)
     total[...] = before[...]
     agg = lambda place: whole[tile_rows(place), :]
-    add_products(late, groups[1], tiles, hidden_rows(features, weights, agg), total)
+    add_products(late, groups[2], tiles, hidden_rows(features, weights, agg), total)
     write_quarters(total, quarters)
 
 
@@ -241,19 +245,18 @@
 def per_device(
     features, tiles, tile_where, tile_count, degree, self_one, neigh_one, self_two, neigh_two
 ):
-    early, late, groups, scale, weights = call(
+    *lists, groups, scale, weights = call(
         plan_kernel,
         (tile_where.reshape(SLOTS, 2).T, tile_count),
         (),
         (degree.reshape(4, 128), self_one, neigh_one),
         [
-            jax.ShapeDtypeStruct((LISTED,), jnp.int32),
-            jax.ShapeDtypeStruct((LISTED,), jnp.int32),
-            jax.ShapeDtypeStruct((2,), jnp.int32),
+            *[jax.ShapeDtypeStruct((LISTED,), jnp.int32)] * 3,
+            jax.ShapeDtypeStruct((3,), jnp.int32),
             jax.ShapeDtypeStruct((128, 128), jnp.float32),
             jax.ShapeDtypeStruct((256, 256), jnp.bfloat16),
         ],
-        [pltpu.SMEM] * 3 + [pltpu.VMEM] * 2,
+        [pltpu.SMEM] * 4 + [pltpu.VMEM] * 2,
         limit=2,
     )
     (tiles_held,) = call(
@@ -275,7 +278,7 @@
     pieces = spread(features)
     *quarters, features_held = call(
         first_kernel,
-        (early, late, groups),
+        (*lists, groups),
         (),
         (tiles_held, *pieces),
         quarter_shapes(128, jnp.float32) + [whole],
@@ -301,19 +304,30 @@
     own_part = jnp.dot(own_hidden, self_two, preferred_element_type=jnp.float32)
 
     pieces = spread(own_agg)
+    part = [jax.ShapeDtypeStruct((3 * TILE, 256), jnp.float32)]
     (total,) = call(
-        second_early,
-        (early, groups),
-        (),
-        (tiles_held, features_held, weights, pieces[0], pieces[3]),
-        [jax.ShapeDtypeStruct((3 * TILE, 256), jnp.float32)],
+        second_first,
+        (lists[0], groups),
+        (),
+        (tiles_held, features_held, weights, pieces[0]),
+        part,
         [pltpu.VMEM],
         limit=4,
-        flops=1 << 30,
+        flops=1 << 29,
+    )
+    (total,) = call(
+        second_second,
+        (lists[1], groups),
+        (),
+        (tiles_held, features_held, weights, total, pieces[3]),
+        part,
+        [pltpu.VMEM],
+        limit=4,
+        flops=1 << 29,
     )
     quarters = call(
         second_late,
-        (late, groups),
+        (lists[2], groups),
         (),
         (tiles_held, features_held, weights, total, *pieces[1:3], *pieces[4:]),
         quarter_shapes(256, jnp.bfloat16),

time: 158 us -> 159 us (level)
    pallas_call x7 -> x8, Pallas kernels: 22 us -> 22.7 us  [call(): pl.pallas_call(kernel, out_shape=outs, in_specs=[space(pltpu.SMEM)] * len...]
where the time goes in v4:
time: 159 us; the launch traced here: 158 us
  starting transfers between devices  69 us (43%)
  waiting for transfers between devices  62.5 us (39%)
  Pallas kernels  22.7 us (14%)
  local copies, waits for them, and re-layouts  2.43 us (2%)
    ppermute x20, starting transfers between devices, hops(): received.append(lax.ppermute(value, PLANE, in_plane(k, phase)))  27 us
    ppermute x20, waiting for transfers between devices, hops(): received.append(lax.ppermute(value, PLANE, in_plane(k, phase)))  24.7 us
    pallas_call x8, Pallas kernels, call(): pl.pallas_call(kernel, out_shape=outs, in_specs=[space(pltpu.SMEM)] * len...  22.7 us
    ppermute x12, waiting for transfers between devices, over_rep(): lax.ppermute(values[k], 'zl', [(i, i ^ k) for i in range(4)])  18.2 us
    ppermute x12, starting transfers between devices, over_rep(): lax.ppermute(values[k], 'zl', [(i, i ^ k) for i in range(4)])  18.2 us
    ppermute x2, starting transfers between devices, spread(): other = lax.ppermute(block, 'zh', SWAP)  12.2 us
    ppermute x4, waiting for transfers between devices, onward(): top = lax.ppermute(one[:half], PLANE, in_plane(1, 1))  9.98 us
    ppermute x4, waiting for transfers between devices, onward(): bottom = lax.ppermute(three[half:], PLANE, in_plane(3, 1))  8.09 us
  transfers between devices with their start and end apart: 48, of which 27 were waited for; matrix products, arithmetic and copies ran while one was open for 2% of the time, Pallas kernels for 6%

profile of v4, /device:TPU:8, one launch (start us, length us, event | category | flops | bytes accessed | tf_op | source)
XLA Modules:
  0.0 158.4 jit_solution(3152166911283681197)
XLA Ops:
  0.0 7.2 %collective-permute-start.5 = (bf16[512,128]{1,0:T(8,128)(2,1)}, bf16[512,128]{1,0:T(8,128)(2,1)S(1)}, u32[]{:S(2)}, u32[]{:S(2)}) collective-permute-start(bf16[512,128]{1,0:T(8,128)(2,1)} %param.9), channel_id=1, source_target_pairs={{0,128},{128,0},{1,129},{129,1},{2,130},{130,2},{3,131},{131,3},{4... | collective-permute-start | bytes 393224 | tf_op jit(solution)/shard_map/ppermute | solution.py:49
  8.7 2.7 %collective-permute-start.2 = (bf16[512,128]{1,0:T(8,128)(2,1)}, bf16[512,128]{1,0:T(8,128)(2,1)S(1)}, u32[]{:S(2)}, u32[]{:S(2)}) collective-permute-start(bf16[512,128]{1,0:T(8,128)(2,1)} %param.9), channel_id=1, source_target_pairs={{0,64},{4,20},{8,72},{12,28},{16,80},{20,4},{24,88},{28,12},{32,96... | collective-permute-start | bytes 393224 | tf_op jit(solution)/shard_map/ppermute | solution.py:37
  18.8 2.3 %collective-permute-start.8 = (bf16[512,128]{1,0:T(8,128)(2,1)S(1)}, bf16[512,128]{1,0:T(8,128)(2,1)S(1)}, u32[]{:S(2)}, u32[]{:S(2)}) collective-permute-start(bf16[512,128]{1,0:T(8,128)(2,1)S(1)} %collective-permute-done.5), channel_id=1, source_target_pairs={{0,64},{4,20},{8,72},{12,28},{16,80},{20,4},{24,88},{28,12},{32,96... | collective-permute-start | bytes 393224 | tf_op jit(solution)/shard_map/ppermute | solution.py:37
  22.8 3.9 %collective-permute-done.7 = bf16[512,128]{1,0:T(8,128)(2,1)S(1)} collective-permute-done((bf16[512,128]{1,0:T(8,128)(2,1)S(1)}, bf16[512,128]{1,0:T(8,128)(2,1)S(1)}, u32[]{:S(2)}, u32[]{:S(2)}) %collective-permute-start.7) | collective-permute-done | bytes 131104 | tf_op jit(solution)/shard_map/ppermute | solution.py:37
  28.9 2.8 %collective-permute-start.12 = (bf16[1024,128]{1,0:T(8,128)(2,1)S(1)}, bf16[1024,128]{1,0:T(8,128)(2,1)S(1)}, u32[]{:S(2)}, u32[]{:S(2)}) collective-permute-start(bf16[1024,128]{1,0:T(8,128)(2,1)S(1)} %slice.33), channel_id=1, source_target_pairs={{0,24},{4,100},{8,0},{12,108},{16,8},{20,116},{24,16},{28,124},{32... | collective-permute-start | bytes 786440 | tf_op jit(solution)/shard_map/ppermute | solution.py:44
  31.8 4.2 %collective-permute-done.9 = bf16[2048,128]{1,0:T(8,128)(2,1)S(1)} collective-permute-done((bf16[2048,128]{1,0:T(8,128)(2,1)S(1)}, bf16[2048,128]{1,0:T(8,128)(2,1)S(1)}, u32[]{:S(2)}, u32[]{:S(2)}) %collective-permute-start.9) | collective-permute-done | bytes 524320 | tf_op jit(solution)/shard_map/ppermute | solution.py:37
  44.2 4.1 %collective-permute-done.13 = bf16[1024,128]{1,0:T(8,128)(2,1)S(1)} collective-permute-done((bf16[1024,128]{1,0:T(8,128)(2,1)S(1)}, bf16[1024,128]{1,0:T(8,128)(2,1)S(1)}, u32[]{:S(2)}, u32[]{:S(2)}) %collective-permute-start.13) | collective-permute-done | bytes 262176 | tf_op jit(solution)/shard_map/ppermute | solution.py:43
  51.3 3.4 %shard_map.92.tiles = bf16[64,256,256]{2,1,0:T(8,128)(2,1)S(1)} custom-call(bf16[64,256,256]{2,1,0:T(8,128)(2,1)} %bitcast.9), custom_call_target="tpu_custom_call" | custom-call | flops 1048576 | bytes 1048576 | tf_op jit(solution)/shard_map/pallas_call | solution.py:209
  54.8 2.4 %shard_map.91 = (s32[68]{0:T(128)S(1)}, s32[68]{0:T(128)S(1)}, s32[68]{0:T(128)S(1)}, s32[3]{0:T(128)S(1)}, f32[128,128]{1,0:T(8,128)S(1)}, /*index=5*/bf16[256,256]{1,0:T(8,128)(2,1)S(1)}) custom-call(s32[2,64]{1,0:T(2,128)S(1)} %bitcast.8, s32[1,1]{1,0:T(1,128)S(6)} %copy.45.count, s32[4,128]{1,0:T(4,128)S(1)} %bitcast.7, bf16[128,256]{1,0:T(8,128)(2,1)S(1)} %copy-done.2, ...), custom_call_target="tpu_custom_call" | custom-call | flops 1048576 | bytes 1048576 | tf_op jit(solution)/shard_map/pallas_call | solution.py:209
  57.2 5.5 %shard_map.93 = (f32[128,128]{1,0:T(8,128)S(1)}, f32[128,128]{1,0:T(8,128)S(1)}, f32[128,128]{1,0:T(8,128)S(1)}, f32[128,128]{1,0:T(8,128)S(1)}, bf16[32768,128]{1,0:T(8,128)(2,1)S(1)}) custom-call(s32[68]{0:T(128)S(1)} %get-tuple-element.20.first.listed, s32[68]{0:T(128)S(1)} %get-tuple-element.21.second.listed, s32[68]{0:T(128)S(1)} %get-tuple-element.22.late, ...), custom_call_target="tpu_custom_call" | custom-call | flops 1073741824 | bytes 1048576 | tf_op jit(solution)/shard_map/pallas_call | solution.py:209
  64.6 2.6 %collective-permute-start.20 = (f32[128,128]{1,0:T(8,128)S(1)}, f32[128,128]{1,0:T(8,128)S(1)}, u32[]{:S(2)}, u32[]{:S(2)}) collective-permute-start(f32[128,128]{1,0:T(8,128)S(1)} %get-tuple-element.27), channel_id=1, source_target_pairs={{0,3},{1,2},{2,1},{3,0},{4,7},{5,6},{6,5},{7,4},{8,11},{9,10},{10,... | collective-permute-start | bytes 196616 | tf_op jit(solution)/shard_map/ppermute | solution.py:229
  67.3 5.0 %collective-permute-done.19 = f32[128,128]{1,0:T(8,128)S(1)} collective-permute-done((f32[128,128]{1,0:T(8,128)S(1)}, f32[128,128]{1,0:T(8,128)S(1)}, u32[]{:S(2)}, u32[]{:S(2)}) %collective-permute-start.19) | collective-permute-done | bytes 65568 | tf_op jit(solution)/shard_map/ppermute | solution.py:229
  79.8 5.1 %collective-permute-start.30 = (bf16[512,128]{1,0:T(8,128)(2,1)S(1)}, bf16[512,128]{1,0:T(8,128)(2,1)S(1)}, u32[]{:S(2)}, u32[]{:S(2)}) collective-permute-start(bf16[512,128]{1,0:T(8,128)(2,1)S(1)} %shard_map.94), channel_id=1, source_target_pairs={{0,128},{128,0},{1,129},{129,1},{2,130},{130,2},{3,131},{131,3},{4... | collective-permute-start | bytes 393224 | tf_op jit(solution)/shard_map/ppermute | solution.py:49
  90.2 2.5 %collective-permute-start.31 = (bf16[512,128]{1,0:T(8,128)(2,1)S(1)}, bf16[512,128]{1,0:T(8,128)(2,1)S(1)}, u32[]{:S(2)}, u32[]{:S(2)}) collective-permute-start(bf16[512,128]{1,0:T(8,128)(2,1)S(1)} %collective-permute-done.30), channel_id=1, source_target_pairs={{0,32},{4,12},{8,40},{12,20},{16,48},{20,28},{24,56},{28,4},{32,64... | collective-permute-start | bytes 393224 | tf_op jit(solution)/shard_map/ppermute | solution.py:37
  98.5 3.5 %collective-permute-done.32 = bf16[512,128]{1,0:T(8,128)(2,1)S(1)} collective-permute-done((bf16[512,128]{1,0:T(8,128)(2,1)S(1)}, bf16[512,128]{1,0:T(8,128)(2,1)S(1)}, u32[]{:S(2)}, u32[]{:S(2)}) %collective-permute-start.32) | collective-permute-done | bytes 131104 | tf_op jit(solution)/shard_map/ppermute | solution.py:37
  105.9 2.6 %collective-permute-start.37 = (bf16[1024,128]{1,0:T(8,128)(2,1)S(1)}, bf16[1024,128]{1,0:T(8,128)(2,1)S(1)}, u32[]{:S(2)}, u32[]{:S(2)}) collective-permute-start(bf16[1024,128]{1,0:T(8,128)(2,1)S(1)} %slice.37), channel_id=1, source_target_pairs={{0,24},{4,100},{8,0},{12,108},{16,8},{20,116},{24,16},{28,124},{32... | collective-permute-start | bytes 786440 | tf_op jit(solution)/shard_map/ppermute | solution.py:44
  108.6 4.2 %collective-permute-done.34 = bf16[2048,128]{1,0:T(8,128)(2,1)S(1)} collective-permute-done((bf16[2048,128]{1,0:T(8,128)(2,1)S(1)}, bf16[2048,128]{1,0:T(8,128)(2,1)S(1)}, u32[]{:S(2)}, u32[]{:S(2)}) %collective-permute-start.34) | collective-permute-done | bytes 524320 | tf_op jit(solution)/shard_map/ppermute | solution.py:37
  120.5 4.2 %collective-permute-done.38 = bf16[1024,128]{1,0:T(8,128)(2,1)S(1)} collective-permute-done((bf16[1024,128]{1,0:T(8,128)(2,1)S(1)}, bf16[1024,128]{1,0:T(8,128)(2,1)S(1)}, u32[]{:S(2)}, u32[]{:S(2)}) %collective-permute-start.38) | collective-permute-done | bytes 262176 | tf_op jit(solution)/shard_map/ppermute | solution.py:43
  127.0 2.4 %shard_map.95.before = f32[768,256]{1,0:T(8,128)S(1)} custom-call(s32[68]{0:T(128)S(1)} %get-tuple-element.20.first.listed, s32[3]{0:T(128)S(1)} %get-tuple-element.23.groups, bf16[64,256,256]{2,1,0:T(8,128)(2,1)S(1)} %shard_map.92.tiles, bf16[32768,128]{1,0:T(8,128)(2,1)S(1)} %get-tuple-element.30.features, bf16[256,256]{1,0:T(8,128)(2,1)S(1)} %get-tuple-element.29.weights, ...), custom_call_target="tpu_custom_call" | custom-call | flops 536870912 | bytes 1048576 | tf_op jit(solution)/shard_map/pallas_call | solution.py:209
  131.4 6.1 %shard_map.97 = (f32[128,256]{1,0:T(8,128)S(1)}, bf16[128,256]{1,0:T(8,128)(2,1)S(1)}, bf16[128,256]{1,0:T(8,128)(2,1)S(1)}, bf16[128,256]{1,0:T(8,128)(2,1)S(1)}) custom-call(s32[68]{0:T(128)S(1)} %get-tuple-element.22.late, s32[3]{0:T(128)S(1)} %get-tuple-element.23.groups, bf16[64,256,256]{2,1,0:T(8,128)(2,1)S(1)} %shard_map.92.tiles, ...), custom_call_target="tpu_custom_call" | custom-call | flops 2147483648 | bytes 1048576 | tf_op jit(solution)/shard_map/pallas_call | solution.py:209
  137.5 2.3 %collective-permute-start.42 = (bf16[128,256]{1,0:T(8,128)(2,1)S(1)}, bf16[128,256]{1,0:T(8,128)(2,1)S(1)}, u32[]{:S(2)}, u32[]{:S(2)}) collective-permute-start(bf16[128,256]{1,0:T(8,128)(2,1)S(1)} %get-tuple-element.32), channel_id=1, source_target_pairs={{0,1},{1,0},{2,3},{3,2},{4,5},{5,4},{6,7},{7,6},{8,9},{9,8},{10,11... | collective-permute-start | bytes 196616 | tf_op jit(solution)/shard_map/ppermute | solution.py:229
  139.8 2.5 %collective-permute-start.44 = (bf16[128,256]{1,0:T(8,128)(2,1)S(1)}, bf16[128,256]{1,0:T(8,128)(2,1)S(1)}, u32[]{:S(2)}, u32[]{:S(2)}) collective-permute-start(bf16[128,256]{1,0:T(8,128)(2,1)S(1)} %get-tuple-element.34), channel_id=1, source_target_pairs={{0,3},{1,2},{2,1},{3,0},{4,7},{5,6},{6,5},{7,4},{8,11},{9,10},{10,... | collective-permute-start | bytes 196616 | tf_op jit(solution)/shard_map/ppermute | solution.py:229
  142.5 5.0 %collective-permute-done.43 = bf16[128,256]{1,0:T(8,128)(2,1)S(1)} collective-permute-done((bf16[128,256]{1,0:T(8,128)(2,1)S(1)}, bf16[128,256]{1,0:T(8,128)(2,1)S(1)}, u32[]{:S(2)}, u32[]{:S(2)}) %collective-permute-start.43) | collective-permute-done | bytes 65568 | tf_op jit(solution)/shard_map/ppermute | solution.py:229
  154.5 2.8 %collective-permute-done.46.refs_2_ = bf16[128,256]{1,0:T(8,128)(2,1)S(1)} collective-permute-done((bf16[128,256]{1,0:T(8,128)(2,1)S(1)}, bf16[128,256]{1,0:T(8,128)(2,1)S(1)}, u32[]{:S(2)}, u32[]{:S(2)}) %collective-permute-start.46) | collective-permute-done | bytes 65568 | tf_op jit(solution)/shard_map/ppermute | solution.py:229
  (138 shorter events, 67.8 us)
Async XLA Ops:
  0.0 13.8 %collective-permute-start.5 = (bf16[512,128]{1,0:T(8,128)(2,1)}, bf16[512,128]{1,0:T(8,128)(2,1)S(1)}, u32[]{:S(2)}, u32[]{:S(2)}) collective-permute-start(bf16[512,128]{1,0:T(8,128)(2,1)} %param.9), channel_id=1, source_target_pairs={{0,128},{128,0},{1,129},{129,1},{2,130},{130,2},{3,131},{131,3},{4... | collective-permute-start | bytes 393224 | tf_op jit(solution)/shard_map/ppermute | solution.py:49
  8.7 8.0 %collective-permute-start.2 = (bf16[512,128]{1,0:T(8,128)(2,1)}, bf16[512,128]{1,0:T(8,128)(2,1)S(1)}, u32[]{:S(2)}, u32[]{:S(2)}) collective-permute-start(bf16[512,128]{1,0:T(8,128)(2,1)} %param.9), channel_id=1, source_target_pairs={{0,64},{4,20},{8,72},{12,28},{16,80},{20,4},{24,88},{28,12},{32,96... | collective-permute-start | bytes 393224 | tf_op jit(solution)/shard_map/ppermute | solution.py:37
  13.8 8.9 %collective-permute-start.6 = (bf16[512,128]{1,0:T(8,128)(2,1)S(1)}, bf16[512,128]{1,0:T(8,128)(2,1)S(1)}, u32[]{:S(2)}, u32[]{:S(2)}) collective-permute-start(bf16[512,128]{1,0:T(8,128)(2,1)S(1)} %collective-permute-done.5), channel_id=1, source_target_pairs={{0,32},{4,12},{8,40},{12,20},{16,48},{20,28},{24,56},{28,4},{32,64... | collective-permute-start | bytes 393224 | tf_op jit(solution)/shard_map/ppermute | solution.py:37
  16.7 12.2 %collective-permute-start.4 = (bf16[2048,128]{1,0:T(8,128)(2,1)S(1)}, bf16[2048,128]{1,0:T(8,128)(2,1)S(1)}, u32[]{:S(2)}, u32[]{:S(2)}) collective-permute-start(bf16[2048,128]{1,0:T(8,128)(2,1)S(1)} %get-tuple-element.51), channel_id=1, source_target_pairs={{0,24},{4,100},{8,0},{12,108},{16,8},{20,116},{24,16},{28,124},{32... | collective-permute-start | bytes 1572872 | tf_op jit(solution)/shard_map/ppermute | solution.py:37
  17.2 14.5 %collective-permute-start.3 = (bf16[2048,128]{1,0:T(8,128)(2,1)S(1)}, bf16[2048,128]{1,0:T(8,128)(2,1)S(1)}, u32[]{:S(2)}, u32[]{:S(2)}) collective-permute-start(bf16[2048,128]{1,0:T(8,128)(2,1)S(1)} %get-tuple-element.51), channel_id=1, source_target_pairs={{0,8},{4,36},{8,16},{12,44},{16,24},{20,52},{24,0},{28,60},{32,40}... | collective-permute-start | bytes 1572872 | tf_op jit(solution)/shard_map/ppermute | solution.py:37
  18.8 7.9 %collective-permute-start.8 = (bf16[512,128]{1,0:T(8,128)(2,1)S(1)}, bf16[512,128]{1,0:T(8,128)(2,1)S(1)}, u32[]{:S(2)}, u32[]{:S(2)}) collective-permute-start(bf16[512,128]{1,0:T(8,128)(2,1)S(1)} %collective-permute-done.5), channel_id=1, source_target_pairs={{0,64},{4,20},{8,72},{12,28},{16,80},{20,4},{24,88},{28,12},{32,96... | collective-permute-start | bytes 393224 | tf_op jit(solution)/shard_map/ppermute | solution.py:37
  26.8 9.3 %collective-permute-start.9 = (bf16[2048,128]{1,0:T(8,128)(2,1)S(1)}, bf16[2048,128]{1,0:T(8,128)(2,1)S(1)}, u32[]{:S(2)}, u32[]{:S(2)}) collective-permute-start(bf16[2048,128]{1,0:T(8,128)(2,1)S(1)} %get-tuple-element.43), channel_id=1, source_target_pairs={{0,8},{4,36},{8,16},{12,44},{16,24},{20,52},{24,0},{28,60},{32,40}... | collective-permute-start | bytes 1572872 | tf_op jit(solution)/shard_map/ppermute | solution.py:37
  28.5 9.6 %collective-permute-start.10 = (bf16[2048,128]{1,0:T(8,128)(2,1)S(1)}, bf16[2048,128]{1,0:T(8,128)(2,1)S(1)}, u32[]{:S(2)}, u32[]{:S(2)}) collective-permute-start(bf16[2048,128]{1,0:T(8,128)(2,1)S(1)} %get-tuple-element.43), channel_id=1, source_target_pairs={{0,24},{4,100},{8,0},{12,108},{16,8},{20,116},{24,16},{28,124},{32... | collective-permute-start | bytes 1572872 | tf_op jit(solution)/shard_map/ppermute | solution.py:37
  28.9 11.9 %collective-permute-start.12 = (bf16[1024,128]{1,0:T(8,128)(2,1)S(1)}, bf16[1024,128]{1,0:T(8,128)(2,1)S(1)}, u32[]{:S(2)}, u32[]{:S(2)}) collective-permute-start(bf16[1024,128]{1,0:T(8,128)(2,1)S(1)} %slice.33), channel_id=1, source_target_pairs={{0,24},{4,100},{8,0},{12,108},{16,8},{20,116},{24,16},{28,124},{32... | collective-permute-start | bytes 786440 | tf_op jit(solution)/shard_map/ppermute | solution.py:44
  40.9 16.3 %collective-permute-start.16 = (bf16[8192,128]{1,0:T(8,128)(2,1)S(1)}, bf16[8192,128]{1,0:T(8,128)(2,1)S(1)}, u32[]{:S(2)}, u32[]{:S(2)}) collective-permute-start(bf16[8192,128]{1,0:T(8,128)(2,1)S(1)} %constant_dynamic-update-slice_fusion.14.refs_1_), channel_id=1, source_target_pairs={{0,4},{4,0},{1,5},{5,1},{2,6},{6,2},{3,7},{7,3},{8,12},{12,8},{9,1... | collective-permute-start | bytes 6291464 | tf_op jit(solution)/shard_map/ppermute | solution.py:59
  41.2 16.1 %collective-permute-start.15 = (bf16[6144,128]{1,0:T(8,128)(2,1)S(1)}, bf16[6144,128]{1,0:T(8,128)(2,1)S(1)}, u32[]{:S(2)}, u32[]{:S(2)}) collective-permute-start(bf16[6144,128]{1,0:T(8,128)(2,1)S(1)} %constant_dynamic-update-slice_fusion.4.refs_0_), channel_id=1, source_target_pairs={{0,4},{4,0},{1,5},{5,1},{2,6},{6,2},{3,7},{7,3},{8,12},{12,8},{9,1... | collective-permute-start | bytes 4718600 | tf_op jit(solution)/shard_map/ppermute | solution.py:59
  79.8 10.4 %collective-permute-start.30 = (bf16[512,128]{1,0:T(8,128)(2,1)S(1)}, bf16[512,128]{1,0:T(8,128)(2,1)S(1)}, u32[]{:S(2)}, u32[]{:S(2)}) collective-permute-start(bf16[512,128]{1,0:T(8,128)(2,1)S(1)} %shard_map.94), channel_id=1, source_target_pairs={{0,128},{128,0},{1,129},{129,1},{2,130},{130,2},{3,131},{131,3},{4... | collective-permute-start | bytes 393224 | tf_op jit(solution)/shard_map/ppermute | solution.py:49
  84.8 7.9 %collective-permute-start.26 = (bf16[512,128]{1,0:T(8,128)(2,1)S(1)}, bf16[512,128]{1,0:T(8,128)(2,1)S(1)}, u32[]{:S(2)}, u32[]{:S(2)}) collective-permute-start(bf16[512,128]{1,0:T(8,128)(2,1)S(1)} %shard_map.94), channel_id=1, source_target_pairs={{0,64},{4,20},{8,72},{12,28},{16,80},{20,4},{24,88},{28,12},{32,96... | collective-permute-start | bytes 393224 | tf_op jit(solution)/shard_map/ppermute | solution.py:37
  90.2 8.3 %collective-permute-start.31 = (bf16[512,128]{1,0:T(8,128)(2,1)S(1)}, bf16[512,128]{1,0:T(8,128)(2,1)S(1)}, u32[]{:S(2)}, u32[]{:S(2)}) collective-permute-start(bf16[512,128]{1,0:T(8,128)(2,1)S(1)} %collective-permute-done.30), channel_id=1, source_target_pairs={{0,32},{4,12},{8,40},{12,20},{16,48},{20,28},{24,56},{28,4},{32,64... | collective-permute-start | bytes 393224 | tf_op jit(solution)/shard_map/ppermute | solution.py:37
  94.6 11.2 %collective-permute-start.28 = (bf16[2048,128]{1,0:T(8,128)(2,1)S(1)}, bf16[2048,128]{1,0:T(8,128)(2,1)S(1)}, u32[]{:S(2)}, u32[]{:S(2)}) collective-permute-start(bf16[2048,128]{1,0:T(8,128)(2,1)S(1)} %pad_maximum_fusion), channel_id=1, source_target_pairs={{0,24},{4,100},{8,0},{12,108},{16,8},{20,116},{24,16},{28,124},{32... | collective-permute-start | bytes 1572872 | tf_op jit(solution)/shard_map/ppermute | solution.py:37
  94.7 13.8 %collective-permute-start.27 = (bf16[2048,128]{1,0:T(8,128)(2,1)S(1)}, bf16[2048,128]{1,0:T(8,128)(2,1)S(1)}, u32[]{:S(2)}, u32[]{:S(2)}) collective-permute-start(bf16[2048,128]{1,0:T(8,128)(2,1)S(1)} %pad_maximum_fusion), channel_id=1, source_target_pairs={{0,8},{4,36},{8,16},{12,44},{16,24},{20,52},{24,0},{28,60},{32,40}... | collective-permute-start | bytes 1572872 | tf_op jit(solution)/shard_map/ppermute | solution.py:37
  103.4 9.5 %collective-permute-start.34 = (bf16[2048,128]{1,0:T(8,128)(2,1)S(1)}, bf16[2048,128]{1,0:T(8,128)(2,1)S(1)}, u32[]{:S(2)}, u32[]{:S(2)}) collective-permute-start(bf16[2048,128]{1,0:T(8,128)(2,1)S(1)} %get-tuple-element.35), channel_id=1, source_target_pairs={{0,8},{4,36},{8,16},{12,44},{16,24},{20,52},{24,0},{28,60},{32,40}... | collective-permute-start | bytes 1572872 | tf_op jit(solution)/shard_map/ppermute | solution.py:37
  105.2 9.4 %collective-permute-start.35 = (bf16[2048,128]{1,0:T(8,128)(2,1)S(1)}, bf16[2048,128]{1,0:T(8,128)(2,1)S(1)}, u32[]{:S(2)}, u32[]{:S(2)}) collective-permute-start(bf16[2048,128]{1,0:T(8,128)(2,1)S(1)} %get-tuple-element.35), channel_id=1, source_target_pairs={{0,24},{4,100},{8,0},{12,108},{16,8},{20,116},{24,16},{28,124},{32... | collective-permute-start | bytes 1572872 | tf_op jit(solution)/shard_map/ppermute | solution.py:37
  105.9 11.5 %collective-permute-start.37 = (bf16[1024,128]{1,0:T(8,128)(2,1)S(1)}, bf16[1024,128]{1,0:T(8,128)(2,1)S(1)}, u32[]{:S(2)}, u32[]{:S(2)}) collective-permute-start(bf16[1024,128]{1,0:T(8,128)(2,1)S(1)} %slice.37), channel_id=1, source_target_pairs={{0,24},{4,100},{8,0},{12,108},{16,8},{20,116},{24,16},{28,124},{32... | collective-permute-start | bytes 786440 | tf_op jit(solution)/shard_map/ppermute | solution.py:44
  117.5 13.9 %collective-permute-start.40 = (bf16[8192,128]{1,0:T(8,128)(2,1)S(1)}, bf16[8192,128]{1,0:T(8,128)(2,1)S(1)}, u32[]{:S(2)}, u32[]{:S(2)}) collective-permute-start(bf16[8192,128]{1,0:T(8,128)(2,1)S(1)} %constant_dynamic-update-slice_fusion.34.refs_0_), channel_id=1, source_target_pairs={{0,4},{4,0},{1,5},{5,1},{2,6},{6,2},{3,7},{7,3},{8,12},{12,8},{9,1... | collective-permute-start | bytes 6291464 | tf_op jit(solution)/shard_map/ppermute | solution.py:59
  117.7 11.7 %collective-permute-start.29 = (bf16[6144,128]{1,0:T(8,128)(2,1)S(1)}, bf16[6144,128]{1,0:T(8,128)(2,1)S(1)}, u32[]{:S(2)}, u32[]{:S(2)}) collective-permute-start(bf16[6144,128]{1,0:T(8,128)(2,1)S(1)} %constant_dynamic-update-slice_fusion.24.piece), channel_id=1, source_target_pairs={{0,4},{4,0},{1,5},{5,1},{2,6},{6,2},{3,7},{7,3},{8,12},{12,8},{9,1... | collective-permute-start | bytes 4718600 | tf_op jit(solution)/shard_map/ppermute | solution.py:59
  139.8 7.8 %collective-permute-start.43 = (bf16[128,256]{1,0:T(8,128)(2,1)S(1)}, bf16[128,256]{1,0:T(8,128)(2,1)S(1)}, u32[]{:S(2)}, u32[]{:S(2)}) collective-permute-start(bf16[128,256]{1,0:T(8,128)(2,1)S(1)} %get-tuple-element.33), channel_id=1, source_target_pairs={{0,2},{1,3},{2,0},{3,1},{4,6},{5,7},{6,4},{7,5},{8,10},{9,11},{10,... | collective-permute-start | bytes 196616 | tf_op jit(solution)/shard_map/ppermute | solution.py:229
  139.8 7.8 %collective-permute-start.44 = (bf16[128,256]{1,0:T(8,128)(2,1)S(1)}, bf16[128,256]{1,0:T(8,128)(2,1)S(1)}, u32[]{:S(2)}, u32[]{:S(2)}) collective-permute-start(bf16[128,256]{1,0:T(8,128)(2,1)S(1)} %get-tuple-element.34), channel_id=1, source_target_pairs={{0,3},{1,2},{2,1},{3,0},{4,7},{5,6},{6,5},{7,4},{8,11},{9,10},{10,... | collective-permute-start | bytes 196616 | tf_op jit(solution)/shard_map/ppermute | solution.py:229
  149.1 8.2 %collective-permute-start.46 = (bf16[128,256]{1,0:T(8,128)(2,1)S(1)}, bf16[128,256]{1,0:T(8,128)(2,1)S(1)}, u32[]{:S(2)}, u32[]{:S(2)}) collective-permute-start(bf16[128,256]{1,0:T(8,128)(2,1)S(1)} %fusion.9.refs_0_), channel_id=1, source_target_pairs={{0,2},{1,3},{2,0},{3,1},{4,6},{5,7},{6,4},{7,5},{8,10},{9,11},{10,... | collective-permute-start | bytes 196616 | tf_op jit(solution)/shard_map/ppermute | solution.py:229
  (31 other events, 360.1 us)
